TPU v7x, 256 devices: a whole 4x4x8 slice. The times are simulated.
256 devices in a mesh: gx: 8 (over x, core), gy: 4 (over y), gz: 8 (over z).
Axes of the slice: x: 4, y: 4, z: 8, core: 2. Of those that a mesh axis runs over, the one named last changes fastest.
Arguments:
- dual_rhs: float32 [8, 4, 8, 3, 300, 128], P('gx', 'gy', 'gz'), may hold values from -6 to 6
- local_flex: bfloat16 [8, 4, 8, 1800, 1800], P('gx', 'gy', 'gz'), as said below
- corner_coupling: bfloat16 [8, 4, 8, 24, 1800], P('gx', 'gy', 'gz'), may hold values from -0.375 to 0.375
- face_stiffness: bfloat16 [8, 4, 8, 6, 300, 300], P('gx', 'gy', 'gz'), as said below
- coarse_inverse: bfloat16 [441, 441], replicated, as said below
- corner_ids: int32 [8, 4, 8, 8], P('gx', 'gy', 'gz'), may hold values from -1 to 146, as said below
Outputs:
- multipliers: float32 [8, 4, 8, 3, 300, 128], P('gx', 'gy', 'gz')
- residual: float32 [8, 4, 8, 3, 300, 128], P('gx', 'gy', 'gz')
Inputs may be any that keep to these rules, and one draw needn't show every extreme that they name: `local_flex`: each subdomain's matrix is symmetric positive definite. `face_stiffness`: each face block is symmetric positive definite. `coarse_inverse`: symmetric positive definite. `corner_ids`: entry k = 4 kx + 2 ky + kz of subdomain (i, j, l) is the number of the corner at lattice point (i + kx, j + ky, l + kz) when that point has all coordinates strictly between 0 and the subdomain counts, else -1; the 147 interior corners are numbered by a permutation, so subdomains sharing a corner name the same node.
All inputs are finite; a program needn't handle non-finite values.
Results may differ from a plain program's by a relative error of at most 0.04.
Values may be sent and summed in bfloat16 or wider, within the bound.
A program may use at most 64 MiB of HBM per device.

v0:
```python
import jax
import jax.numpy as jnp
from jax import lax
from jax.sharding import Mesh
from jax.sharding import PartitionSpec as P

ITERS = 3
GX = ("gx_0", "gx_1")


def with_halo(value, sides, width):
    for axis, dim in sides:
        size, length = (lax.axis_size(axis), value.shape[dim])
        up = [(i, (i + 1) % size) for i in range(size - 1)]
        down = [(j, i) for i, j in up]
        last = lax.slice_in_dim(value, length - width, length, axis=dim)
        first = lax.slice_in_dim(value, 0, width, axis=dim)
        before = lax.ppermute(last, axis, up)
        after = lax.ppermute(first, axis, down)
        value = jnp.concatenate([before, value, after], axis=dim)
    return value


def from_everyone(value, axis):
    copies = jnp.broadcast_to(value, (lax.axis_size(axis), *value.shape))
    return lax.all_to_all(copies, axis, split_axis=0, concat_axis=0, tiled=True)


def of_everyone(value, axis):
    return from_everyone(value, axis).sum(axis=0)


def over_axes(value, axes):
    far, near = axes
    nearer = of_everyone(value, near)
    return of_everyone(nearer, far)


def in_blocks(value, dim, size):
    lengths = value.shape
    pieces = value.reshape(*lengths[:dim], size, lengths[dim] // size, *lengths[dim + 1 :])
    return jnp.moveaxis(pieces, dim, 0)


def sum_at_owner(value, axis, dim):
    pieces = in_blocks(value, dim, lax.axis_size(axis))
    arrived = lax.all_to_all(pieces, axis, split_axis=0, concat_axis=0, tiled=True)
    return arrived.astype(jnp.float32).sum(axis=0)


def summed_rows(value, axes, dim):
    far, near = axes
    pieces = in_blocks(value, dim, lax.axis_size(far))
    nearer = sum_at_owner(pieces, near, dim + 1)
    arrived = lax.all_to_all(
        nearer.astype(jnp.bfloat16), far, split_axis=0, concat_axis=0, tiled=True
    )
    return arrived.astype(jnp.float32).sum(axis=0)


def filled_up(lines, size):
    spare = -len(lines) % size
    return jnp.pad(lines, [(0, spare)] + [(0, 0)] * (lines.ndim - 1))


def in_order(pieces, dim):
    lengths = list(pieces.shape[1:])
    lengths[dim] *= pieces.shape[0]
    return jnp.moveaxis(pieces, 0, dim).reshape(lengths)


def whole_of(value, axes, dim):
    far, near = axes
    first = from_everyone(value, far)
    pieces = jnp.swapaxes(from_everyone(first, near), 0, 1)
    return in_order(pieces.reshape(-1, *value.shape), dim)


def sum_by_parts(value, axes):
    lines = value.reshape(-1)
    own = summed_rows(filled_up(lines, lax.axis_size(axes[0]) * lax.axis_size(axes[1])), axes, 0)
    whole = whole_of(own.astype(jnp.bfloat16), axes, 0)
    return whole[: len(lines)].reshape(value.shape).astype(jnp.float32)


def face_neighbours(face_pairs):
    along_x = with_halo(face_pairs[0].astype(jnp.bfloat16), ((GX, 0),), 1).astype(jnp.float32)
    along_y = with_halo(face_pairs[1].astype(jnp.bfloat16), (("gy", 0),), 1).astype(jnp.float32)
    along_z = with_halo(face_pairs[2].astype(jnp.bfloat16), (("gz", 0),), 1).astype(jnp.float32)
    return [along_x, along_y, along_z]


def face_jump(values, face_mask):
    extended = face_neighbours([values[0:2], values[2:4], values[4:6]])
    face_list = []
    for bordered in extended:
        face_list.append(bordered[0] - bordered[1])
        face_list.append(bordered[2] - bordered[3])
    return jnp.stack(face_list) * face_mask[:, None, None]


def duplicate(owned, face_mask):
    empty = jnp.zeros_like(owned[0])
    extended = face_neighbours([jnp.stack([empty, owned[axis_pos]]) for axis_pos in range(3)])
    face_list = []
    for axis_pos in range(3):
        face_list.append(extended[axis_pos][0])
        face_list.append(owned[axis_pos])
    return jnp.stack(face_list) * face_mask[:, None, None]


def neighbour_stiffness(stiffness):
    along_x = with_halo(stiffness[0:2], ((GX, 0),), 1)
    along_y = with_halo(stiffness[2:4], (("gy", 0),), 1)
    along_z = with_halo(stiffness[4:6], (("gz", 0),), 1)
    return jnp.stack([along_x[0], along_x[3], along_y[0], along_y[3], along_z[0], along_z[3]])


def owned_inner(left, right):
    return jnp.sum(left[1::2] * right[1::2], axis=(0, 1))


def global_sum(local_value):
    return over_axes(local_value, (("gx_0", "gx_1"), ("gy", "gz")))


def body(dual_rhs, local_flex, corner_coupling, face_stiffness, coarse_inverse, corner_ids):
    owned_rhs = dual_rhs[0, 0, 0]
    flex = local_flex[0, 0, 0]
    coupling = corner_coupling[0, 0, 0]
    stiffness = face_stiffness[0, 0, 0]
    corner_list = corner_ids[0, 0, 0]
    face_count, face_width, columns = (stiffness.shape[0], stiffness.shape[1], owned_rhs.shape[2])
    coarse_rows = coarse_inverse.shape[0]
    face_sign = jnp.array([-1.0, 1.0, -1.0, 1.0, -1.0, 1.0], jnp.float32)[:, None, None]
    place_x = lax.axis_index(GX)
    place_y = lax.axis_index("gy")
    place_z = lax.axis_index("gz")
    face_mask = jnp.stack(
        [
            place_x > 0,
            place_x < lax.axis_size(GX) - 1,
            place_y > 0,
            place_y < lax.axis_size("gy") - 1,
            place_z > 0,
            place_z < lax.axis_size("gz") - 1,
        ]
    ).astype(jnp.float32)
    coupling_wide = coupling.astype(jnp.float32)
    dof_ids = jnp.where(
        corner_list[:, None] >= 0,
        3 * corner_list[:, None] + jnp.arange(3, dtype=jnp.int32)[None, :],
        -1,
    ).reshape(-1)
    assembly = (jnp.arange(coarse_rows, dtype=jnp.int32)[:, None] == dof_ids[None, :]).astype(
        jnp.float32
    )
    beyond = neighbour_stiffness(stiffness)

    def precondition(dual):
        halved = (0.5 * face_sign * dual).astype(jnp.bfloat16)
        own_part = jnp.einsum("fij,fjr->fir", stiffness, halved, preferred_element_type=jnp.float32)
        far_part = jnp.einsum("fij,fjr->fir", beyond, halved, preferred_element_type=jnp.float32)
        return 0.5 * face_sign * (own_part + far_part) * face_mask[:, None, None]

    residual = duplicate(owned_rhs, face_mask)
    multiplier = jnp.zeros_like(residual)
    precond_res = precondition(residual)
    rho_now = global_sum(owned_inner(residual, precond_res))
    direction = precond_res
    for iteration in range(ITERS):
        signed = (
            (face_sign * direction).astype(jnp.bfloat16).reshape(face_count * face_width, columns)
        )
        local_local_image = jnp.dot(flex, signed, preferred_element_type=jnp.float32)
        corner_part = jnp.dot(coupling, signed, preferred_element_type=jnp.float32)
        coarse_part = jnp.dot(assembly, corner_part, precision=lax.Precision.HIGHEST)
        dual_coarse_rhs = sum_by_parts(
            coarse_part.astype(jnp.bfloat16), (("gx_0", "gx_1"), ("gy", "gz"))
        )
        coarse_sol = jnp.dot(
            coarse_inverse, dual_coarse_rhs.astype(jnp.bfloat16), preferred_element_type=jnp.float32
        )
        corner_sol = lax.dot_general(
            assembly, coarse_sol, (((0,), (0,)), ((), ())), precision=lax.Precision.HIGHEST
        )
        displaced = local_local_image + lax.dot_general(
            coupling_wide, corner_sol, (((0,), (0,)), ((), ())), precision=lax.Precision.HIGHEST
        )
        curvature = global_sum(jnp.sum(signed.astype(jnp.float32) * displaced, axis=0))
        image = face_jump(displaced.reshape(face_count, face_width, columns), face_mask)
        image, curvature = (image, curvature)
        step_size = rho_now / curvature
        multiplier = multiplier + step_size * direction
        residual = residual - step_size * image
        if iteration + 1 < ITERS:
            precond_res = precondition(residual)
            rho_next = global_sum(owned_inner(residual, precond_res))
            direction = precond_res + rho_next / rho_now * direction
            rho_now = rho_next
    return (multiplier[1::2][None, None, None], residual[1::2][None, None, None])


def solution(mesh):
    torus = Mesh(
        mesh.devices.reshape(4, 2, mesh.shape["gy"], mesh.shape["gz"]), ("gx_0", "gx_1", "gy", "gz")
    )
    in_specs = (
        P(GX, "gy", "gz", None, None, None),
        P(GX, "gy", "gz", None, None),
        P(GX, "gy", "gz", None, None),
        P(GX, "gy", "gz", None, None, None),
        P(),
        P(GX, "gy", "gz", None),
    )
    out_specs = (P(GX, "gy", "gz", None, None, None), P(GX, "gy", "gz", None, None, None))
    return jax.shard_map(body, mesh=torus, in_specs=in_specs, out_specs=out_specs, check_vma=False)
```

profile of v0, /device:TPU:1, one launch (start us, length us, event | category | flops | bytes accessed | tf_op | source)
XLA Modules:
  0.0 401.6 jit_solution(9360596173612316954)
XLA Ops:
  2.5 4.5 %collective-permute-start = (bf16[1,300,128]{2,1,0:T(8,128)(2,1)}, bf16[1,300,128]{2,1,0:T(8,128)(2,1)}, u32[]{:S(2)}, u32[]{:S(2)}) collective-permute-start(bf16[1,300,128]{2,1,0:T(8,128)(2,1)} %bitcast.185), channel_id=1, source_target_pairs={{0,32},{32,64},{64,96},{96,128},{128,160},{160,192},{192,224},{1,3... | collective-permute-start | bytes 230408 | tf_op jit(solution)/shard_map/ppermute | solution.py:18
  7.6 3.8 collective-permute-start.1
  12.1 4.3 %collective-permute-start.2 = (bf16[1,300,128]{2,1,0:T(8,128)(2,1)}, bf16[1,300,128]{2,1,0:T(8,128)(2,1)}, u32[]{:S(2)}, u32[]{:S(2)}) collective-permute-start(bf16[1,300,128]{2,1,0:T(8,128)(2,1)} %bitcast.187), channel_id=1, source_target_pairs={{0,1},{1,2},{2,3},{3,4},{4,5},{5,6},{6,7},{8,9},{9,10},{10,11},{11... | collective-permute-start | bytes 230408 | tf_op jit(solution)/shard_map/ppermute | solution.py:18
  27.8 2.9 collective-permute-start.7
  36.2 6.8 %collective-permute-done.8 = bf16[1,300,300]{2,1,0:T(8,128)(2,1)S(1)} collective-permute-done((bf16[1,300,300]{2,1,0:T(8,128)(2,1)S(1)}, bf16[1,300,300]{2,1,0:T(8,128)(2,1)S(1)}, u32[]{:S(2)}, u32[]{:S(2)}) %collective-permute-start.8) | collective-permute-done | bytes 180032 | tf_op jit(solution)/shard_map/ppermute | solution.py:19
  48.5 19.0 %all_to_all.156 = bf16[32,8,221]{2,1,0:T(8,128)(2,1)S(1)} all-to-all(bf16[32,8,221]{2,1,0:T(8,128)(2,1)S(1)} %copy.60), channel_id=1, replica_groups=mesh['gx_0'=4,'gx_1'=2,'gy'=4,'gz'=8] {'gy','gz'}, dimensions={0} | all-to-all | bytes 226304 | tf_op jit(solution)/shard_map/all_to_all | solution.py:47
  68.1 6.5 %all-to-all-start.3 = ((bf16[8,1,221]{2,1,0:T(2,128)(2,1)}), bf16[8,1,221]{2,1,0:T(2,128)(2,1)S(1)}, u32[]{:S(2)}, u32[]{:S(2)}) async-start(bf16[8,1,221]{2,1,0:T(2,128)(2,1)} %copy.61), calls=%async_computation.3 | async-start | bytes 16384 | tf_op jit(solution)/shard_map/all_to_all | solution.py:55
  75.8 3.5 all-to-all-done.3
  79.8 3.8 all-to-all-start
  83.7 8.6 %all-to-all-done = f32[32,1,128]{2,1,0:T(1,128)S(1)} async-done(((f32[32,1,128]{2,1,0:T(1,128)}), f32[32,1,128]{2,1,0:T(1,128)S(1)}, u32[]{:S(2)}, u32[]{:S(2)}) %all-to-all-start) | async-done | bytes 16416 | tf_op jit(solution)/shard_map/all_to_all | solution.py:26
  92.9 5.1 %all-to-all-start.4 = ((bf16[8,1,221]{2,1,0:T(2,128)(2,1)}), bf16[8,1,221]{2,1,0:T(2,128)(2,1)S(1)}, u32[]{:S(2)}, u32[]{:S(2)}) async-start(bf16[8,1,221]{2,1,0:T(2,128)(2,1)} %broadcast_in_dim.94), calls=%async_computation.4 | async-start | bytes 16384 | tf_op jit(solution)/shard_map/all_to_all | solution.py:26
  98.0 4.6 %all-to-all-done.4 = bf16[8,1,221]{2,1,0:T(2,128)(2,1)S(1)} async-done(((bf16[8,1,221]{2,1,0:T(2,128)(2,1)}), bf16[8,1,221]{2,1,0:T(2,128)(2,1)S(1)}, u32[]{:S(2)}, u32[]{:S(2)}) %all-to-all-start.4) | async-done | bytes 3568 | tf_op jit(solution)/shard_map/all_to_all | solution.py:26
  103.2 3.9 all-to-all-start.1
  107.1 4.5 %all-to-all-done.1 = f32[8,1,128]{2,1,0:T(1,128)S(1)} async-done(((f32[8,1,128]{2,1,0:T(1,128)}), f32[8,1,128]{2,1,0:T(1,128)S(1)}, u32[]{:S(2)}, u32[]{:S(2)}) %all-to-all-start.1) | async-done | bytes 4128 | tf_op jit(solution)/shard_map/all_to_all | solution.py:26
  112.3 3.9 all-to-all-start.5
  116.2 6.0 %fusion.4 = f32[128,1800]{0,1:T(8,128)} fusion(bf16[1800,128]{1,0:T(8,128)(2,1)S(1)} %reshape.266, bf16[1,1,1,1800,1800]{4,3,2,1,0:T(8,128)(2,1)} %param.8), kind=kOutput, calls=%fused_computation.4 | convolution fusion | flops 829440000 | bytes 7862400 | tf_op jit(solution)/shard_map/dot_general | solution.py:175
  122.2 3.1 all-to-all-done.5
  128.5 6.1 %all-to-all-start.6 = ((f32[32,1,128]{2,1,0:T(1,128)}), f32[32,1,128]{2,1,0:T(1,128)S(1)}, u32[]{:S(2)}, u32[]{:S(2)}) async-start(f32[32,1,128]{2,1,0:T(1,128)} %broadcast_in_dim.96), calls=%async_computation.6 | async-start | bytes 32768 | tf_op jit(solution)/shard_map/all_to_all | solution.py:26
  135.3 3.2 collective-permute-start.10
  143.8 5.6 %all-to-all-start.7 = ((f32[8,1,128]{2,1,0:T(1,128)}), f32[8,1,128]{2,1,0:T(1,128)S(1)}, u32[]{:S(2)}, u32[]{:S(2)}) async-start(f32[8,1,128]{2,1,0:T(1,128)} %broadcast_in_dim.97), calls=%async_computation.7 | async-start | bytes 8192 | tf_op jit(solution)/shard_map/all_to_all | solution.py:26
  150.8 4.0 collective-permute-start.11
  156.2 4.2 %collective-permute-start.13 = (bf16[1,300,128]{2,1,0:T(8,128)(2,1)S(1)}, bf16[1,300,128]{2,1,0:T(8,128)(2,1)S(1)}, u32[]{:S(2)}, u32[]{:S(2)}) collective-permute-start(bf16[1,300,128]{2,1,0:T(8,128)(2,1)S(1)} %get-tuple-element.44), channel_id=1, source_target_pairs={{0,1},{1,2},{2,3},{3,4},{4,5},{5,6},{6,7},{8,9},{9,10},{10,11},{11... | collective-permute-start | bytes 230408 | tf_op jit(solution)/shard_map/ppermute | solution.py:18
  164.6 15.1 %all_to_all.157 = f32[32,1,128]{2,1,0:T(1,128)S(1)} all-to-all(f32[32,1,128]{2,1,0:T(1,128)S(1)} %broadcast_in_dim.98), channel_id=1, replica_groups=mesh['gx_0'=4,'gx_1'=2,'gy'=4,'gz'=8] {'gy','gz'}, dimensions={0} | all-to-all | bytes 32768 | tf_op jit(solution)/shard_map/all_to_all | solution.py:26
  179.7 12.6 %all_to_all.158 = f32[8,1,128]{2,1,0:T(1,128)S(1)} all-to-all(f32[8,1,128]{2,1,0:T(1,128)S(1)} %broadcast_in_dim.99), channel_id=1, replica_groups=mesh['gx_0'=4,'gx_1'=2,'gy'=4,'gz'=8] {'gx_0','gx_1'}, dimensions={0} | all-to-all | bytes 8192 | tf_op jit(solution)/shard_map/all_to_all | solution.py:26
  198.1 12.1 %all_to_all.159 = bf16[32,8,221]{2,1,0:T(8,128)(2,1)S(1)} all-to-all(bf16[32,8,221]{2,1,0:T(8,128)(2,1)S(1)} %copy.67), channel_id=1, replica_groups=mesh['gx_0'=4,'gx_1'=2,'gy'=4,'gz'=8] {'gy','gz'}, dimensions={0} | all-to-all | bytes 226304 | tf_op jit(solution)/shard_map/all_to_all | solution.py:47
  210.3 9.1 %all_to_all.160 = bf16[8,1,221]{2,1,0:T(2,128)(2,1)S(1)} all-to-all(bf16[8,1,221]{2,1,0:T(2,128)(2,1)S(1)} %copy.68), channel_id=1, replica_groups=mesh['gx_0'=4,'gx_1'=2,'gy'=4,'gz'=8] {'gx_0','gx_1'}, dimensions={0} | all-to-all | bytes 7072 | tf_op jit(solution)/shard_map/all_to_all | solution.py:55
  219.4 7.7 %all_to_all.161 = bf16[8,1,221]{2,1,0:T(2,128)(2,1)S(1)} all-to-all(bf16[8,1,221]{2,1,0:T(2,128)(2,1)S(1)} %broadcast_in_dim.100), channel_id=1, replica_groups=mesh['gx_0'=4,'gx_1'=2,'gy'=4,'gz'=8] {'gx_0','gx_1'}, dimensions={0} | all-to-all | bytes 7072 | tf_op jit(solution)/shard_map/all_to_all | solution.py:26
  227.8 3.9 all-to-all-start.13
  231.6 6.0 %fusion.2 = f32[128,1800]{0,1:T(8,128)} fusion(bf16[1800,128]{1,0:T(8,128)(2,1)S(1)} %reshape.268, bf16[1,1,1,1800,1800]{4,3,2,1,0:T(8,128)(2,1)} %param.8), kind=kOutput, calls=%fused_computation.2 | convolution fusion | flops 829440000 | bytes 7862400 | tf_op jit(solution)/shard_map/dot_general | solution.py:175
  237.6 3.1 all-to-all-done.13
  246.3 6.1 %all-to-all-start.14 = ((f32[32,1,128]{2,1,0:T(1,128)}), f32[32,1,128]{2,1,0:T(1,128)S(1)}, u32[]{:S(2)}, u32[]{:S(2)}) async-start(f32[32,1,128]{2,1,0:T(1,128)} %broadcast_in_dim.102), calls=%async_computation.14 | async-start | bytes 32768 | tf_op jit(solution)/shard_map/all_to_all | solution.py:26
  254.2 3.2 collective-permute-start.16
  261.6 5.6 %all-to-all-start.15 = ((f32[8,1,128]{2,1,0:T(1,128)}), f32[8,1,128]{2,1,0:T(1,128)S(1)}, u32[]{:S(2)}, u32[]{:S(2)}) async-start(f32[8,1,128]{2,1,0:T(1,128)} %broadcast_in_dim.103), calls=%async_computation.15 | async-start | bytes 8192 | tf_op jit(solution)/shard_map/all_to_all | solution.py:26
  270.3 4.6 %collective-permute-start.17 = (bf16[1,300,128]{2,1,0:T(8,128)(2,1)}, bf16[1,300,128]{2,1,0:T(8,128)(2,1)}, u32[]{:S(2)}, u32[]{:S(2)}) collective-permute-start(bf16[1,300,128]{2,1,0:T(8,128)(2,1)} %get-tuple-element.38), channel_id=1, source_target_pairs={{0,8},{8,16},{16,24},{1,9},{9,17},{17,25},{2,10},{10,18},{18,26},{... | collective-permute-start | bytes 230408 | tf_op jit(solution)/shard_map/ppermute | solution.py:18
  277.3 4.0 collective-permute-start.19
  288.1 16.0 %all_to_all.162 = f32[32,1,128]{2,1,0:T(1,128)S(1)} all-to-all(f32[32,1,128]{2,1,0:T(1,128)S(1)} %broadcast_in_dim.104), channel_id=1, replica_groups=mesh['gx_0'=4,'gx_1'=2,'gy'=4,'gz'=8] {'gy','gz'}, dimensions={0} | all-to-all | bytes 32768 | tf_op jit(solution)/shard_map/all_to_all | solution.py:26
  304.1 12.6 %all_to_all.163 = f32[8,1,128]{2,1,0:T(1,128)S(1)} all-to-all(f32[8,1,128]{2,1,0:T(1,128)S(1)} %broadcast_in_dim.105), channel_id=1, replica_groups=mesh['gx_0'=4,'gx_1'=2,'gy'=4,'gz'=8] {'gx_0','gx_1'}, dimensions={0} | all-to-all | bytes 8192 | tf_op jit(solution)/shard_map/all_to_all | solution.py:26
  319.2 12.1 %all_to_all.164 = bf16[32,8,221]{2,1,0:T(8,128)(2,1)S(1)} all-to-all(bf16[32,8,221]{2,1,0:T(8,128)(2,1)S(1)} %copy.74), channel_id=1, replica_groups=mesh['gx_0'=4,'gx_1'=2,'gy'=4,'gz'=8] {'gy','gz'}, dimensions={0} | all-to-all | bytes 226304 | tf_op jit(solution)/shard_map/all_to_all | solution.py:47
  331.4 9.1 %all_to_all.165 = bf16[8,1,221]{2,1,0:T(2,128)(2,1)S(1)} all-to-all(bf16[8,1,221]{2,1,0:T(2,128)(2,1)S(1)} %copy.75), channel_id=1, replica_groups=mesh['gx_0'=4,'gx_1'=2,'gy'=4,'gz'=8] {'gx_0','gx_1'}, dimensions={0} | all-to-all | bytes 7072 | tf_op jit(solution)/shard_map/all_to_all | solution.py:55
  340.5 7.7 %all_to_all.166 = bf16[8,1,221]{2,1,0:T(2,128)(2,1)S(1)} all-to-all(bf16[8,1,221]{2,1,0:T(2,128)(2,1)S(1)} %broadcast_in_dim.106), channel_id=1, replica_groups=mesh['gx_0'=4,'gx_1'=2,'gy'=4,'gz'=8] {'gx_0','gx_1'}, dimensions={0} | all-to-all | bytes 7072 | tf_op jit(solution)/shard_map/all_to_all | solution.py:26
  348.9 3.9 all-to-all-start.21
  352.7 6.0 %fusion = f32[128,1800]{0,1:T(8,128)} fusion(bf16[1800,128]{1,0:T(8,128)(2,1)S(1)} %reshape.270, bf16[1,1,1,1800,1800]{4,3,2,1,0:T(8,128)(2,1)} %param.8), kind=kOutput, calls=%fused_computation | convolution fusion | flops 829440000 | bytes 7862400 | tf_op jit(solution)/shard_map/dot_general | solution.py:175
  358.7 3.1 all-to-all-done.21
  365.0 6.1 %all-to-all-start.22 = ((f32[32,1,128]{2,1,0:T(1,128)}), f32[32,1,128]{2,1,0:T(1,128)S(1)}, u32[]{:S(2)}, u32[]{:S(2)}) async-start(f32[32,1,128]{2,1,0:T(1,128)} %broadcast_in_dim.108), calls=%async_computation.22 | async-start | bytes 32768 | tf_op jit(solution)/shard_map/all_to_all | solution.py:26
  371.2 3.2 collective-permute-start.22
  380.3 5.6 %all-to-all-start.23 = ((f32[8,1,128]{2,1,0:T(1,128)}), f32[8,1,128]{2,1,0:T(1,128)S(1)}, u32[]{:S(2)}, u32[]{:S(2)}) async-start(f32[8,1,128]{2,1,0:T(1,128)} %broadcast_in_dim.109), calls=%async_computation.23 | async-start | bytes 8192 | tf_op jit(solution)/shard_map/all_to_all | solution.py:26
  387.4 4.0 collective-permute-start.23
  392.8 4.0 collective-permute-start.25
  (257 shorter events, 95.4 us)
Async XLA Ops:
  0.6 125.1 %copy-start = (bf16[441,441]{1,0:T(8,128)(2,1)S(1)}, bf16[441,441]{1,0:T(8,128)(2,1)}, u32[]{:S(2)}) copy-start(bf16[441,441]{1,0:T(8,128)(2,1)} %param.11) | copy-start | bytes 1166890
  0.6 15.8 %copy-start.1 = (bf16[1,1,1,6,300,300]{5,4,3,2,1,0:T(8,128)(2,1)S(1)}, bf16[1,1,1,6,300,300]{5,4,3,2,1,0:T(8,128)(2,1)}, u32[]{:S(2)}) copy-start(bf16[1,1,1,6,300,300]{5,4,3,2,1,0:T(8,128)(2,1)} %param.10) | copy-start | bytes 3240004
  2.5 19.5 %collective-permute-start = (bf16[1,300,128]{2,1,0:T(8,128)(2,1)}, bf16[1,300,128]{2,1,0:T(8,128)(2,1)}, u32[]{:S(2)}, u32[]{:S(2)}) collective-permute-start(bf16[1,300,128]{2,1,0:T(8,128)(2,1)} %bitcast.185), channel_id=1, source_target_pairs={{0,32},{32,64},{64,96},{96,128},{128,160},{160,192},{192,224},{1,3... | collective-permute-start | bytes 230408 | tf_op jit(solution)/shard_map/ppermute | solution.py:18
  7.6 17.9 %collective-permute-start.1 = (bf16[1,300,128]{2,1,0:T(8,128)(2,1)}, bf16[1,300,128]{2,1,0:T(8,128)(2,1)}, u32[]{:S(2)}, u32[]{:S(2)}) collective-permute-start(bf16[1,300,128]{2,1,0:T(8,128)(2,1)} %bitcast.186), channel_id=1, source_target_pairs={{0,8},{8,16},{16,24},{1,9},{9,17},{17,25},{2,10},{10,18},{18,26},{... | collective-permute-start | bytes 230408 | tf_op jit(solution)/shard_map/ppermute | solution.py:18
  12.1 9.6 %copy-start.23 = (s32[1,1,1,8]{3,2,1,0:T(1,128)S(1)}, s32[1,1,1,8]{3,2,1,0:T(1,128)}, u32[]{:S(2)}) copy-start(s32[1,1,1,8]{3,2,1,0:T(1,128)} %param.12) | copy-start | bytes 100
  12.1 15.7 %collective-permute-start.2 = (bf16[1,300,128]{2,1,0:T(8,128)(2,1)}, bf16[1,300,128]{2,1,0:T(8,128)(2,1)}, u32[]{:S(2)}, u32[]{:S(2)}) collective-permute-start(bf16[1,300,128]{2,1,0:T(8,128)(2,1)} %bitcast.187), channel_id=1, source_target_pairs={{0,1},{1,2},{2,3},{3,4},{4,5},{5,6},{6,7},{8,9},{9,10},{10,11},{11... | collective-permute-start | bytes 230408 | tf_op jit(solution)/shard_map/ppermute | solution.py:18
  17.3 16.1 %collective-permute-start.3 = (bf16[1,300,300]{2,1,0:T(8,128)(2,1)}, bf16[1,300,300]{2,1,0:T(8,128)(2,1)S(1)}, u32[]{:S(2)}, u32[]{:S(2)}) collective-permute-start(bf16[1,300,300]{2,1,0:T(8,128)(2,1)} %get-tuple-element.18), channel_id=1, source_target_pairs={{0,32},{32,64},{64,96},{96,128},{128,160},{160,192},{192,224},{1,3... | collective-permute-start | bytes 540008 | tf_op jit(solution)/shard_map/ppermute | solution.py:18
  19.8 14.9 %collective-permute-start.4 = (bf16[1,300,300]{2,1,0:T(8,128)(2,1)}, bf16[1,300,300]{2,1,0:T(8,128)(2,1)S(1)}, u32[]{:S(2)}, u32[]{:S(2)}) collective-permute-start(bf16[1,300,300]{2,1,0:T(8,128)(2,1)} %get-tuple-element.17), channel_id=1, source_target_pairs={{32,0},{64,32},{96,64},{128,96},{160,128},{192,160},{224,192},{33,... | collective-permute-start | bytes 540008 | tf_op jit(solution)/shard_map/ppermute | solution.py:19
  22.0 12.8 %collective-permute-start.5 = (bf16[1,300,300]{2,1,0:T(8,128)(2,1)}, bf16[1,300,300]{2,1,0:T(8,128)(2,1)S(1)}, u32[]{:S(2)}, u32[]{:S(2)}) collective-permute-start(bf16[1,300,300]{2,1,0:T(8,128)(2,1)} %get-tuple-element.16), channel_id=1, source_target_pairs={{0,8},{8,16},{16,24},{1,9},{9,17},{17,25},{2,10},{10,18},{18,26},{... | collective-permute-start | bytes 540008 | tf_op jit(solution)/shard_map/ppermute | solution.py:18
  25.5 9.5 %collective-permute-start.6 = (bf16[1,300,300]{2,1,0:T(8,128)(2,1)S(1)}, bf16[1,300,300]{2,1,0:T(8,128)(2,1)S(1)}, u32[]{:S(2)}, u32[]{:S(2)}) collective-permute-start(bf16[1,300,300]{2,1,0:T(8,128)(2,1)S(1)} %get-tuple-element.15), channel_id=1, source_target_pairs={{8,0},{16,8},{24,16},{9,1},{17,9},{25,17},{10,2},{18,10},{26,18},{... | collective-permute-start | bytes 540008 | tf_op jit(solution)/shard_map/ppermute | solution.py:19
  27.7 5.0 %copy-start.21 = (f32[6]{0:T(128)S(1)}, f32[6]{0:T(128)}, u32[]{:S(2)}) copy-start(f32[6]{0:T(128)} %constant.57) | copy-start | bytes 76
  27.8 8.4 %collective-permute-start.7 = (bf16[1,300,300]{2,1,0:T(8,128)(2,1)S(1)}, bf16[1,300,300]{2,1,0:T(8,128)(2,1)S(1)}, u32[]{:S(2)}, u32[]{:S(2)}) collective-permute-start(bf16[1,300,300]{2,1,0:T(8,128)(2,1)S(1)} %get-tuple-element.19), channel_id=1, source_target_pairs={{0,1},{1,2},{2,3},{3,4},{4,5},{5,6},{6,7},{8,9},{9,10},{10,11},{11... | collective-permute-start | bytes 540008 | tf_op jit(solution)/shard_map/ppermute | solution.py:18
  32.8 10.3 %copy-start.14 = (f32[6,300,128]{2,1,0:T(8,128)}, f32[6,300,128]{2,1,0:T(8,128)S(1)}, u32[]{:S(2)}) copy-start(f32[6,300,128]{2,1,0:T(8,128)S(1)} %broadcast_multiply_fusion) | copy-start | bytes 2764804
  33.4 9.7 %copy-start.22 = (f32[6]{0:T(128)S(1)}, f32[6]{0:T(128)}, u32[]{:S(2)}) copy-start(f32[6]{0:T(128)} %constant.45.clone) | copy-start | bytes 76
  33.4 9.6 %collective-permute-start.8 = (bf16[1,300,300]{2,1,0:T(8,128)(2,1)S(1)}, bf16[1,300,300]{2,1,0:T(8,128)(2,1)S(1)}, u32[]{:S(2)}, u32[]{:S(2)}) collective-permute-start(bf16[1,300,300]{2,1,0:T(8,128)(2,1)S(1)} %get-tuple-element.14), channel_id=1, source_target_pairs={{1,0},{2,1},{3,2},{4,3},{5,4},{6,5},{7,6},{9,8},{10,9},{11,10},{12... | collective-permute-start | bytes 540008 | tf_op jit(solution)/shard_map/ppermute | solution.py:19
  44.6 31.2 %copy-start.4 = (f32[6,300,128]{2,1,0:T(8,128)}, f32[6,300,128]{2,1,0:T(8,128)S(1)}, u32[]{:S(2)}) copy-start(f32[6,300,128]{2,1,0:T(8,128)S(1)} %get-tuple-element.59) | copy-start | bytes 2764804
  68.1 11.1 %all-to-all-start.3 = ((bf16[8,1,221]{2,1,0:T(2,128)(2,1)}), bf16[8,1,221]{2,1,0:T(2,128)(2,1)S(1)}, u32[]{:S(2)}, u32[]{:S(2)}) async-start(bf16[8,1,221]{2,1,0:T(2,128)(2,1)} %copy.61), calls=%async_computation.3 | async-start | bytes 16384 | tf_op jit(solution)/shard_map/all_to_all | solution.py:55
  79.8 12.4 %all-to-all-start = ((f32[32,1,128]{2,1,0:T(1,128)}), f32[32,1,128]{2,1,0:T(1,128)S(1)}, u32[]{:S(2)}, u32[]{:S(2)}) async-start(f32[32,1,128]{2,1,0:T(1,128)} %broadcast_in_dim.90), calls=%async_computation | async-start | bytes 32768 | tf_op jit(solution)/shard_map/all_to_all | solution.py:26
  92.9 9.7 %all-to-all-start.4 = ((bf16[8,1,221]{2,1,0:T(2,128)(2,1)}), bf16[8,1,221]{2,1,0:T(2,128)(2,1)S(1)}, u32[]{:S(2)}, u32[]{:S(2)}) async-start(bf16[8,1,221]{2,1,0:T(2,128)(2,1)} %broadcast_in_dim.94), calls=%async_computation.4 | async-start | bytes 16384 | tf_op jit(solution)/shard_map/all_to_all | solution.py:26
  103.2 8.5 %all-to-all-start.1 = ((f32[8,1,128]{2,1,0:T(1,128)}), f32[8,1,128]{2,1,0:T(1,128)S(1)}, u32[]{:S(2)}, u32[]{:S(2)}) async-start(f32[8,1,128]{2,1,0:T(1,128)} %broadcast_in_dim.91), calls=%async_computation.1 | async-start | bytes 8192 | tf_op jit(solution)/shard_map/all_to_all | solution.py:26
  112.3 13.0 %all-to-all-start.5 = ((bf16[32,8,221]{2,1,0:T(8,128)(2,1)}), bf16[32,8,221]{2,1,0:T(8,128)(2,1)S(1)}, u32[]{:S(2)}, u32[]{:S(2)}) async-start(bf16[32,8,221]{2,1,0:T(8,128)(2,1)} %broadcast_in_dim.95), calls=%async_computation.5 | async-start | bytes 262144 | tf_op jit(solution)/shard_map/all_to_all | solution.py:26
  128.5 14.7 %all-to-all-start.6 = ((f32[32,1,128]{2,1,0:T(1,128)}), f32[32,1,128]{2,1,0:T(1,128)S(1)}, u32[]{:S(2)}, u32[]{:S(2)}) async-start(f32[32,1,128]{2,1,0:T(1,128)} %broadcast_in_dim.96), calls=%async_computation.6 | async-start | bytes 32768 | tf_op jit(solution)/shard_map/all_to_all | solution.py:26
  135.3 21.0 %collective-permute-start.10 = (bf16[1,300,128]{2,1,0:T(8,128)(2,1)}, bf16[1,300,128]{2,1,0:T(8,128)(2,1)S(1)}, u32[]{:S(2)}, u32[]{:S(2)}) collective-permute-start(bf16[1,300,128]{2,1,0:T(8,128)(2,1)} %get-tuple-element.48), channel_id=1, source_target_pairs={{32,0},{64,32},{96,64},{128,96},{160,128},{192,160},{224,192},{33,... | collective-permute-start | bytes 230408 | tf_op jit(solution)/shard_map/ppermute | solution.py:19
  138.4 22.0 %collective-permute-start.9 = (bf16[1,300,128]{2,1,0:T(8,128)(2,1)S(1)}, bf16[1,300,128]{2,1,0:T(8,128)(2,1)S(1)}, u32[]{:S(2)}, u32[]{:S(2)}) collective-permute-start(bf16[1,300,128]{2,1,0:T(8,128)(2,1)S(1)} %get-tuple-element.49), channel_id=1, source_target_pairs={{0,32},{32,64},{64,96},{96,128},{128,160},{160,192},{192,224},{1,3... | collective-permute-start | bytes 230408 | tf_op jit(solution)/shard_map/ppermute | solution.py:18
  143.8 12.4 %all-to-all-start.7 = ((f32[8,1,128]{2,1,0:T(1,128)}), f32[8,1,128]{2,1,0:T(1,128)S(1)}, u32[]{:S(2)}, u32[]{:S(2)}) async-start(f32[8,1,128]{2,1,0:T(1,128)} %broadcast_in_dim.97), calls=%async_computation.7 | async-start | bytes 8192 | tf_op jit(solution)/shard_map/all_to_all | solution.py:26
  149.5 11.0 %collective-permute-start.12 = (bf16[1,300,128]{2,1,0:T(8,128)(2,1)S(1)}, bf16[1,300,128]{2,1,0:T(8,128)(2,1)S(1)}, u32[]{:S(2)}, u32[]{:S(2)}) collective-permute-start(bf16[1,300,128]{2,1,0:T(8,128)(2,1)S(1)} %get-tuple-element.46), channel_id=1, source_target_pairs={{8,0},{16,8},{24,16},{9,1},{17,9},{25,17},{10,2},{18,10},{26,18},{... | collective-permute-start | bytes 230408 | tf_op jit(solution)/shard_map/ppermute | solution.py:19
  150.8 9.7 %collective-permute-start.11 = (bf16[1,300,128]{2,1,0:T(8,128)(2,1)S(1)}, bf16[1,300,128]{2,1,0:T(8,128)(2,1)S(1)}, u32[]{:S(2)}, u32[]{:S(2)}) collective-permute-start(bf16[1,300,128]{2,1,0:T(8,128)(2,1)S(1)} %get-tuple-element.47), channel_id=1, source_target_pairs={{0,8},{8,16},{16,24},{1,9},{9,17},{17,25},{2,10},{10,18},{18,26},{... | collective-permute-start | bytes 230408 | tf_op jit(solution)/shard_map/ppermute | solution.py:18
  154.8 5.8 %collective-permute-start.14 = (bf16[1,300,128]{2,1,0:T(8,128)(2,1)S(1)}, bf16[1,300,128]{2,1,0:T(8,128)(2,1)S(1)}, u32[]{:S(2)}, u32[]{:S(2)}) collective-permute-start(bf16[1,300,128]{2,1,0:T(8,128)(2,1)S(1)} %get-tuple-element.45), channel_id=1, source_target_pairs={{1,0},{2,1},{3,2},{4,3},{5,4},{6,5},{7,6},{9,8},{10,9},{11,10},{12... | collective-permute-start | bytes 230408 | tf_op jit(solution)/shard_map/ppermute | solution.py:19
  156.2 5.4 %collective-permute-start.13 = (bf16[1,300,128]{2,1,0:T(8,128)(2,1)S(1)}, bf16[1,300,128]{2,1,0:T(8,128)(2,1)S(1)}, u32[]{:S(2)}, u32[]{:S(2)}) collective-permute-start(bf16[1,300,128]{2,1,0:T(8,128)(2,1)S(1)} %get-tuple-element.44), channel_id=1, source_target_pairs={{0,1},{1,2},{2,3},{3,4},{4,5},{5,6},{6,7},{8,9},{9,10},{10,11},{11... | collective-permute-start | bytes 230408 | tf_op jit(solution)/shard_map/ppermute | solution.py:18
  227.8 13.0 %all-to-all-start.13 = ((bf16[32,8,221]{2,1,0:T(8,128)(2,1)}), bf16[32,8,221]{2,1,0:T(8,128)(2,1)S(1)}, u32[]{:S(2)}, u32[]{:S(2)}) async-start(bf16[32,8,221]{2,1,0:T(8,128)(2,1)} %broadcast_in_dim.101), calls=%async_computation.13 | async-start | bytes 262144 | tf_op jit(solution)/shard_map/all_to_all | solution.py:26
  246.3 14.7 %all-to-all-start.14 = ((f32[32,1,128]{2,1,0:T(1,128)}), f32[32,1,128]{2,1,0:T(1,128)S(1)}, u32[]{:S(2)}, u32[]{:S(2)}) async-start(f32[32,1,128]{2,1,0:T(1,128)} %broadcast_in_dim.102), calls=%async_computation.14 | async-start | bytes 32768 | tf_op jit(solution)/shard_map/all_to_all | solution.py:26
  254.2 23.1 %collective-permute-start.16 = (bf16[1,300,128]{2,1,0:T(8,128)(2,1)}, bf16[1,300,128]{2,1,0:T(8,128)(2,1)}, u32[]{:S(2)}, u32[]{:S(2)}) collective-permute-start(bf16[1,300,128]{2,1,0:T(8,128)(2,1)} %get-tuple-element.39), channel_id=1, source_target_pairs={{32,0},{64,32},{96,64},{128,96},{160,128},{192,160},{224,192},{33,... | collective-permute-start | bytes 230408 | tf_op jit(solution)/shard_map/ppermute | solution.py:19
  257.4 23.9 %collective-permute-start.15 = (bf16[1,300,128]{2,1,0:T(8,128)(2,1)}, bf16[1,300,128]{2,1,0:T(8,128)(2,1)}, u32[]{:S(2)}, u32[]{:S(2)}) collective-permute-start(bf16[1,300,128]{2,1,0:T(8,128)(2,1)} %get-tuple-element.40), channel_id=1, source_target_pairs={{0,32},{32,64},{64,96},{96,128},{128,160},{160,192},{192,224},{1,3... | collective-permute-start | bytes 230408 | tf_op jit(solution)/shard_map/ppermute | solution.py:18
  261.6 15.6 %all-to-all-start.15 = ((f32[8,1,128]{2,1,0:T(1,128)}), f32[8,1,128]{2,1,0:T(1,128)S(1)}, u32[]{:S(2)}, u32[]{:S(2)}) async-start(f32[8,1,128]{2,1,0:T(1,128)} %broadcast_in_dim.103), calls=%async_computation.15 | async-start | bytes 8192 | tf_op jit(solution)/shard_map/all_to_all | solution.py:26
  269.0 13.3 %collective-permute-start.18 = (bf16[1,300,128]{2,1,0:T(8,128)(2,1)}, bf16[1,300,128]{2,1,0:T(8,128)(2,1)}, u32[]{:S(2)}, u32[]{:S(2)}) collective-permute-start(bf16[1,300,128]{2,1,0:T(8,128)(2,1)} %get-tuple-element.37), channel_id=1, source_target_pairs={{8,0},{16,8},{24,16},{9,1},{17,9},{25,17},{10,2},{18,10},{26,18},{... | collective-permute-start | bytes 230408 | tf_op jit(solution)/shard_map/ppermute | solution.py:19
  270.3 12.0 %collective-permute-start.17 = (bf16[1,300,128]{2,1,0:T(8,128)(2,1)}, bf16[1,300,128]{2,1,0:T(8,128)(2,1)}, u32[]{:S(2)}, u32[]{:S(2)}) collective-permute-start(bf16[1,300,128]{2,1,0:T(8,128)(2,1)} %get-tuple-element.38), channel_id=1, source_target_pairs={{0,8},{8,16},{16,24},{1,9},{9,17},{17,25},{2,10},{10,18},{18,26},{... | collective-permute-start | bytes 230408 | tf_op jit(solution)/shard_map/ppermute | solution.py:18
  275.0 8.4 %collective-permute-start.20 = (bf16[1,300,128]{2,1,0:T(8,128)(2,1)}, bf16[1,300,128]{2,1,0:T(8,128)(2,1)}, u32[]{:S(2)}, u32[]{:S(2)}) collective-permute-start(bf16[1,300,128]{2,1,0:T(8,128)(2,1)} %get-tuple-element.36), channel_id=1, source_target_pairs={{1,0},{2,1},{3,2},{4,3},{5,4},{6,5},{7,6},{9,8},{10,9},{11,10},{12... | collective-permute-start | bytes 230408 | tf_op jit(solution)/shard_map/ppermute | solution.py:19
  277.3 6.1 %collective-permute-start.19 = (bf16[1,300,128]{2,1,0:T(8,128)(2,1)S(1)}, bf16[1,300,128]{2,1,0:T(8,128)(2,1)S(1)}, u32[]{:S(2)}, u32[]{:S(2)}) collective-permute-start(bf16[1,300,128]{2,1,0:T(8,128)(2,1)S(1)} %get-tuple-element.35), channel_id=1, source_target_pairs={{0,1},{1,2},{2,3},{3,4},{4,5},{5,6},{6,7},{8,9},{9,10},{10,11},{11... | collective-permute-start | bytes 230408 | tf_op jit(solution)/shard_map/ppermute | solution.py:18
  287.1 29.6 %copy-start.5 = (f32[6,300,128]{2,1,0:T(8,128)S(1)}, f32[6,300,128]{2,1,0:T(8,128)}, u32[]{:S(2)}) copy-start(f32[6,300,128]{2,1,0:T(8,128)} %copy-done.4) | copy-start | bytes 2764804
  348.9 13.0 %all-to-all-start.21 = ((bf16[32,8,221]{2,1,0:T(8,128)(2,1)}), bf16[32,8,221]{2,1,0:T(8,128)(2,1)S(1)}, u32[]{:S(2)}, u32[]{:S(2)}) async-start(bf16[32,8,221]{2,1,0:T(8,128)(2,1)} %broadcast_in_dim.107), calls=%async_computation.21 | async-start | bytes 262144 | tf_op jit(solution)/shard_map/all_to_all | solution.py:26
  365.0 14.7 %all-to-all-start.22 = ((f32[32,1,128]{2,1,0:T(1,128)}), f32[32,1,128]{2,1,0:T(1,128)S(1)}, u32[]{:S(2)}, u32[]{:S(2)}) async-start(f32[32,1,128]{2,1,0:T(1,128)} %broadcast_in_dim.108), calls=%async_computation.22 | async-start | bytes 32768 | tf_op jit(solution)/shard_map/all_to_all | solution.py:26
  371.2 21.6 %collective-permute-start.22 = (bf16[1,300,128]{2,1,0:T(8,128)(2,1)S(1)}, bf16[1,300,128]{2,1,0:T(8,128)(2,1)S(1)}, u32[]{:S(2)}, u32[]{:S(2)}) collective-permute-start(bf16[1,300,128]{2,1,0:T(8,128)(2,1)S(1)} %get-tuple-element.30), channel_id=1, source_target_pairs={{32,0},{64,32},{96,64},{128,96},{160,128},{192,160},{224,192},{33,... | collective-permute-start | bytes 230408 | tf_op jit(solution)/shard_map/ppermute | solution.py:19
  374.4 22.4 %collective-permute-start.21 = (bf16[1,300,128]{2,1,0:T(8,128)(2,1)S(1)}, bf16[1,300,128]{2,1,0:T(8,128)(2,1)S(1)}, u32[]{:S(2)}, u32[]{:S(2)}) collective-permute-start(bf16[1,300,128]{2,1,0:T(8,128)(2,1)S(1)} %get-tuple-element.31), channel_id=1, source_target_pairs={{0,32},{32,64},{64,96},{96,128},{128,160},{160,192},{192,224},{1,3... | collective-permute-start | bytes 230408 | tf_op jit(solution)/shard_map/ppermute | solution.py:18
  380.3 12.4 %all-to-all-start.23 = ((f32[8,1,128]{2,1,0:T(1,128)}), f32[8,1,128]{2,1,0:T(1,128)S(1)}, u32[]{:S(2)}, u32[]{:S(2)}) async-start(f32[8,1,128]{2,1,0:T(1,128)} %broadcast_in_dim.109), calls=%async_computation.23 | async-start | bytes 8192 | tf_op jit(solution)/shard_map/all_to_all | solution.py:26
  386.0 10.9 %collective-permute-start.24 = (bf16[1,300,128]{2,1,0:T(8,128)(2,1)S(1)}, bf16[1,300,128]{2,1,0:T(8,128)(2,1)S(1)}, u32[]{:S(2)}, u32[]{:S(2)}) collective-permute-start(bf16[1,300,128]{2,1,0:T(8,128)(2,1)S(1)} %get-tuple-element.28), channel_id=1, source_target_pairs={{8,0},{16,8},{24,16},{9,1},{17,9},{25,17},{10,2},{18,10},{26,18},{... | collective-permute-start | bytes 230408 | tf_op jit(solution)/shard_map/ppermute | solution.py:19
  387.4 9.5 %collective-permute-start.23 = (bf16[1,300,128]{2,1,0:T(8,128)(2,1)S(1)}, bf16[1,300,128]{2,1,0:T(8,128)(2,1)S(1)}, u32[]{:S(2)}, u32[]{:S(2)}) collective-permute-start(bf16[1,300,128]{2,1,0:T(8,128)(2,1)S(1)} %get-tuple-element.29), channel_id=1, source_target_pairs={{0,8},{8,16},{16,24},{1,9},{9,17},{17,25},{2,10},{10,18},{18,26},{... | collective-permute-start | bytes 230408 | tf_op jit(solution)/shard_map/ppermute | solution.py:18
  391.4 5.7 %collective-permute-start.26 = (bf16[1,300,128]{2,1,0:T(8,128)(2,1)S(1)}, bf16[1,300,128]{2,1,0:T(8,128)(2,1)S(1)}, u32[]{:S(2)}, u32[]{:S(2)}) collective-permute-start(bf16[1,300,128]{2,1,0:T(8,128)(2,1)S(1)} %get-tuple-element.27), channel_id=1, source_target_pairs={{1,0},{2,1},{3,2},{4,3},{5,4},{6,5},{7,6},{9,8},{10,9},{11,10},{12... | collective-permute-start | bytes 230408 | tf_op jit(solution)/shard_map/ppermute | solution.py:19
  392.8 5.4 %collective-permute-start.25 = (bf16[1,300,128]{2,1,0:T(8,128)(2,1)S(1)}, bf16[1,300,128]{2,1,0:T(8,128)(2,1)S(1)}, u32[]{:S(2)}, u32[]{:S(2)}) collective-permute-start(bf16[1,300,128]{2,1,0:T(8,128)(2,1)S(1)} %get-tuple-element.26), channel_id=1, source_target_pairs={{0,1},{1,2},{2,3},{3,4},{4,5},{5,6},{6,7},{8,9},{9,10},{10,11},{11... | collective-permute-start | bytes 230408 | tf_op jit(solution)/shard_map/ppermute | solution.py:18
  (16 other events, 25.0 us)
where the time goes:
time: 405 us; the launch traced here: 402 us
  starting transfers between devices  140 us (35%)
  blocking collectives  133 us (33%)
  waiting for transfers between devices  47.3 us (12%)
  local copies, waits for them, and re-layouts  36.8 us (9%)
  matrix products  29.4 us (7%)
  other arithmetic  12.8 us (3%)
    all_to_all x6, blocking collectives, from_everyone(): return lax.all_to_all(copies, axis, split_axis=0, concat_axis=0, tiled=True)  71.7 us
    all_to_all x12, starting transfers between devices, from_everyone(): return lax.all_to_all(copies, axis, split_axis=0, concat_axis=0, tiled=True)  59.5 us
    ppermute x15, starting transfers between devices, with_halo(): before = lax.ppermute(last, axis, up)  52.6 us
    all_to_all x3, blocking collectives, sum_at_owner(): lax.all_to_all(pieces, axis, split_axis=0, concat_axis=0, tiled=True)  43.2 us
    all_to_all x12, waiting for transfers between devices, from_everyone(): return lax.all_to_all(copies, axis, split_axis=0, concat_axis=0, tiled=True)  33.6 us
    ppermute x12, starting transfers between devices, with_halo(): after = lax.ppermute(first, axis, down)  21.7 us
    all_to_all x2, blocking collectives, summed_rows(): lax.all_to_all(nearer.astype(jnp.bfloat16), far, split_axis=0, concat_axi...  18.2 us
    dot_general x3, matrix products, body(): jnp.dot(flex, signed, preferred_element_type=jnp.float32)  18 us
  transfers between devices with their start and end apart: 40, of which 15 were waited for; matrix products, arithmetic and copies ran while one was open for 9% of the time, Pallas kernels for 0%

commit v1 on v0

v1 whole, which is shorter than its diff:
```python
import functools

import jax
import jax.numpy as jnp
import numpy as np
from jax import lax
from jax.experimental import pallas as pl
from jax.experimental.pallas import tpu as pltpu
from jax.sharding import PartitionSpec as P

ITERS = 3
MESH = pl.DeviceIdType.MESH
F32 = jnp.float32
BF16 = jnp.bfloat16


def up_to(value, step):
    return -(-value // step) * step


def iota(shape, dim):
    return lax.broadcasted_iota(jnp.int32, shape, dim)


def dot(left, right, contract=None):
    if contract is None:
        contract = (left.ndim - 1, 0)
    dims = (((contract[0],), (contract[1],)), ((), ()))
    return lax.dot_general(left, right, dims, preferred_element_type=F32)


class Sizes:
    def __init__(self, grid, face, cases, coarse):
        self.grid, self.face, self.cases, self.coarse = grid, face, cases, coarse
        self.dofs = 6 * face
        self.wide = up_to(self.dofs, 128)
        self.window = up_to(face + 127, 128)
        nx, ny, nz = grid
        self.plane = (nx - 1) * (ny - 1)
        self.block = up_to(3 * self.plane + 1, 16)
        self.names = up_to(self.plane, 16)
        self.level = self.block + self.names
        self.rows = up_to(self.block * (nz - 1), 128)
        self.lines = nx * ny
        self.chips = nx // 2 * ny


def plane_sums(sz):
    nx, ny, _ = sz.grid
    table = np.zeros((sz.level, sz.lines * 16), np.float32)
    for i in range(nx):
        for j in range(ny):
            for kx in range(2):
                for ky in range(2):
                    x, y = i + kx, j + ky
                    if not (1 <= x < nx and 1 <= y < ny):
                        continue
                    spot = (x - 1) * (ny - 1) + y - 1
                    first = (i * ny + j) * 16
                    for d in range(3):
                        table[d * sz.plane + spot, first + (kx * 2 + ky) * 3 + d] = 1
                    table[sz.block + spot, first + 12 + kx * 2 + ky] = 1
    return table


def corner_order():
    table = np.zeros((32, 24), np.float32)
    for kx in range(2):
        for ky in range(2):
            for kz in range(2):
                for d in range(3):
                    row = kz * 16 + (kx * 2 + ky) * 3 + d
                    table[row, 3 * (4 * kx + 2 * ky + kz) + d] = 1
    return table


def kernel(sz, ids, rhs_h, flex_h, coup_h, stiff_h, inv_h, sums_h, order_h,
           x_ref, res_ref,
           rhs, flex, coup, stiff, inv, sums, order,
           rhs_b, rhs_n, stiff_n, cs, cn, own_t, nb_t, wide_t, ksum,
           r, s, u, p, sg, sgb, loc, cpb, rxy, lev, hb, hn, bmat, ae, pm, pa,
           ss, sx, sy, sp,
           load_sem, i_send, k_recv, r_recv, c_recv,
           xy_send, xy_recv, z_send, z_recv, pp_send, pp_recv, h_send, h_recv,
           sx_send, sx_recv, sy_send, sy_recv, sp_send, sp_recv):
    nx, ny, nz = sz.grid
    face, dofs = sz.face, sz.dofs
    i, j, l = lax.axis_index("gx"), lax.axis_index("gy"), lax.axis_index("gz")
    core = lax.rem(i, 2)
    place = (i, j, l)
    partner = {"gx": i + 1 - 2 * core, "gy": j, "gz": l}

    def toward(f):
        axis, step = f // 2, f % 2
        size = sz.grid[axis]
        spot = list(place)
        spot[axis] = lax.rem(spot[axis] + (1 if step else size - 1), size)
        return dict(zip(("gx", "gy", "gz"), spot))

    def far(di, dj):
        return min(di, nx - di) / 2 + min(dj, ny - dj)

    spread = sorted(
        [(di, dj) for di in range(nx) for dj in range(ny) if di or dj],
        key=lambda t: -far(*t),
    )
    chips = [(di, dj) for di, dj in spread if di % 2 == 0]
    lanes = sorted(range(1, nz), key=lambda t: -min(t, nz - t))

    def across(di, dj):
        return {"gx": lax.rem(i + di, nx), "gy": lax.rem(j + dj, ny), "gz": l}

    def along(dl):
        return {"gx": i, "gy": j, "gz": lax.rem(l + dl, nz)}

    def remote(src, dst, send, recv, target):
        return pltpu.make_async_remote_copy(
            src_ref=src, dst_ref=dst, send_sem=send, recv_sem=recv,
            device_id=target, device_id_type=MESH,
        )

    loads = []
    for n, (src, dst) in enumerate(
        ((stiff_h, stiff), (rhs_h, rhs), (coup_h, coup), (order_h, order),
         (flex_h, flex), (sums_h, sums), (inv_h, inv))
    ):
        copy = pltpu.make_async_copy(src, dst, load_sem.at[n])
        copy.start()
        loads.append(copy)

    barrier = pltpu.get_barrier_semaphore()
    for di, dj in spread:
        pl.semaphore_signal(barrier, inc=1, device_id=across(di, dj), device_id_type=MESH)
    for dl in lanes:
        pl.semaphore_signal(barrier, inc=1, device_id=along(dl), device_id_type=MESH)

    loads[1].wait()
    for a in range(3):
        rhs_b[a] = rhs[a].astype(BF16)
    loads[0].wait()
    pl.semaphore_wait(barrier, len(spread) + len(lanes))

    sent = []

    def send(src, dst, send_sem, recv_sem, target):
        copy = remote(src, dst, send_sem, recv_sem, target)
        copy.start()
        return copy

    for a in range(3):
        sent.append(send(rhs_b.at[a], rhs_n.at[a], i_send.at[a], r_recv.at[a], toward(2 * a + 1)))
    for f in range(6):
        sent.append(send(stiff.at[f], stiff_n.at[f ^ 1], i_send.at[3 + f], k_recv.at[f ^ 1], toward(f)))

    loads[2].wait()
    loads[3].wait()
    cs[...] = jnp.zeros_like(cs)
    cs[:, 0:dofs] = dot(order[...], coup[...]).astype(BF16)
    sgb[...] = jnp.zeros_like(sgb)
    starts = [face * f // 128 * 128 for f in range(6)]
    for f in range(6):
        sent.append(
            send(cs.at[:, pl.ds(starts[f], sz.window)], cn.at[f ^ 1], i_send.at[9 + f],
                 c_recv.at[f ^ 1], toward(f))
        )
    pick_row, pick_col = iota((32, 128), 0), iota((32, 128), 1)
    pick_own = ((pick_col & 63) == pick_row).astype(F32).astype(BF16)
    pick_nb = -((pick_col & 63) == pick_row + 32).astype(F32).astype(BF16)
    own_t[...] = dot(cs[...], pick_own, (0, 0))

    g_rows = 7 * 32
    line = iota((g_rows, 128), 0)
    g, kz, e = line >> 5, (line >> 4) & 1, line & 15
    t = (e * 11) >> 5
    d, kx, ky = e - 3 * t, t >> 1, t & 1

    def shift(minus, plus):
        return (g == plus).astype(jnp.int32) - (g == minus).astype(jnp.int32)

    gx = i + kx + shift(1, 2)
    gy = j + ky + shift(3, 4)
    gz = l + kz + shift(5, 6)
    inside = (e < 12) & (gx >= 1) & (gx < nx) & (gy >= 1) & (gy < ny) & (gz >= 1) & (gz < nz)
    spot = jnp.where(
        inside, sz.block * (gz - 1) + sz.plane * d + (ny - 1) * (gx - 1) + gy - 1, -1
    )
    for k in range(sz.rows // 128):
        ae[sz.rows:sz.rows + g_rows, 128 * k:128 * k + 128] = (
            (iota((g_rows, 128), 1) + 128 * k == spot).astype(F32).astype(BF16)
        )

    masks = []
    for f in range(6):
        axis, step = f // 2, f % 2
        edge = place[axis] < sz.grid[axis] - 1 if step else place[axis] > 0
        masks.append(jnp.where(edge, 1.0, 0.0).astype(F32))
    signs = [-1.0, 1.0] * 3

    def precondition(f):
        u[f] = (0.25 * masks[f]) * dot(ksum[f], r[f].astype(BF16))

    for a in range(3):
        r[2 * a + 1] = rhs[a] * masks[2 * a + 1]
        sent[a].wait_recv()
        r[2 * a] = rhs_n[a].astype(F32) * masks[2 * a]
    for f in range(6):
        remote(stiff.at[f], stiff_n.at[f], i_send.at[3 + f], k_recv.at[f], toward(f)).wait_recv()
        ksum[f] = (stiff[f].astype(F32) + stiff_n[f].astype(F32)).astype(BF16)
        precondition(f)

    def total(count, piece, send_sem, recv_sem):
        return remote(piece, piece, send_sem, recv_sem, partner)

    alpha = beta = gamma_old = curve = None
    for it in range(ITERS):
        last = it + 1 == ITERS
        tall = sz.level if it == 0 else sz.block
        for f in range(6):
            sg[face * f:face * f + face, :] = signs[f] * u[f]
        sgb[0:dofs, :] = sg[...].astype(BF16)
        cp = dot(cs[...], sgb[...])
        if it == 0:
            name = jnp.full((32, sz.cases), ids[7], jnp.int32).astype(F32)
            cp = jnp.where(iota((32, sz.cases), 0) == 31, name, cp)
        low, high = cp[0:16].astype(BF16), cp[16:32].astype(BF16)
        cpb[it, 0] = low
        cpb[it, 1] = high
        slot = i * ny + j
        for di, dj in spread:
            target = across(di, dj)
            send(cpb.at[it, lax.rem(target["gx"], 2)], rxy.at[it, slot], xy_send.at[it],
                 xy_recv.at[it], target)
        rxy[it, slot] = jnp.where(core == 0, low.astype(F32), high.astype(F32)).astype(BF16)

        gamma = sum(jnp.sum(r[f] * u[f], axis=0, keepdims=True) for f in (1, 3, 5))
        if it:
            cross = sum(jnp.sum(s[f] * u[f], axis=0, keepdims=True) for f in (1, 3, 5))
        else:
            cross = jnp.zeros_like(gamma)
        if it == 0:
            loads[4].wait()
        loc[...] = dot(flex[...], sgb[0:dofs, :])
        for f in range(6):
            hb[it, f] = loc[face * f:face * f + face, :].astype(BF16)
        delta = jnp.sum(sgb[0:dofs, :].astype(F32) * loc[...], axis=0, keepdims=True)

        where = iota((8, sz.cases), 0)
        packed = jnp.where(where == 0, gamma, jnp.where(where == 1, cross, jnp.where(where == 2, delta, 0.0)))
        chip = i // 2 * ny + j
        ss[it, 0] = packed
        sx[it, chip] = packed
        for di, dj in chips:
            send(ss.at[it, 0], sx.at[it, chip], sx_send.at[it], sx_recv.at[it], across(di, dj))
        for f in range(6):
            send(hb.at[it, f], hn.at[it, f ^ 1], h_send.at[it], h_recv.at[it], toward(f))

        if it == 0:
            loads[5].wait()
        total(0, rxy.at[it, pl.ds(0, sz.lines - 1)], xy_send.at[it], xy_recv.at[it]).wait_recv()
        lev[it, core, l] = dot(sums[...], rxy[it].reshape(sz.lines * 16, sz.cases)).astype(BF16)
        for dl in lanes:
            piece = lev.at[it, core, l, pl.ds(0, tall)]
            send(piece, piece, z_send.at[it], z_recv.at[it], along(dl))

        total(0, sx.at[it, pl.ds(0, sz.chips - 1)], sx_send.at[it], sx_recv.at[it]).wait_recv()
        packed = jnp.sum(sx[it], axis=0)
        ss[it, 1] = packed
        sy[it, l] = packed
        for dl in lanes:
            send(ss.at[it, 1], sy.at[it, l], sy_send.at[it], sy_recv.at[it], along(dl))

        if it == 0:
            for f in range(6):
                remote(cs.at[:, pl.ds(starts[f], sz.window)], cn.at[f], i_send.at[9 + f],
                       c_recv.at[f], toward(f)).wait_recv()
                nb_t[...] = dot(cn[f], pick_nb, (0, 0))
                off = face * (f ^ 1) - starts[f ^ 1]
                wide_t[f] = (own_t[face * f:face * f + face, :] + nb_t[off:off + face, :]).astype(BF16)

        total(0, sy.at[it, pl.ds(0, nz - 1)], sy_send.at[it], sy_recv.at[it]).wait_recv()
        mine = jnp.sum(sy[it], axis=0)
        ss[it, 2] = mine
        send(ss.at[it, 2], sp.at[it], sp_send.at[it], sp_recv.at[it], partner)

        total(0, lev.at[it, 0, pl.ds(0, nz - 1), pl.ds(0, tall)], z_send.at[it], z_recv.at[it]).wait_recv()
        piece = lev.at[it, core, pl.ds(0, nz), pl.ds(0, tall)]
        send(piece, piece, pp_send.at[it], pp_recv.at[it], partner)
        total(0, piece, pp_send.at[it], pp_recv.at[it]).wait_recv()

        if it == 0:
            bmat[...] = jnp.zeros_like(bmat)
            small_r, small_c = iota((sz.block, sz.names), 0), iota((sz.block, sz.names), 1)
            part = (small_r >= sz.plane).astype(jnp.int32) + (small_r >= 2 * sz.plane).astype(jnp.int32)
            expand = ((small_c == small_r - sz.plane * part) & (small_r < 3 * sz.plane)).astype(F32).astype(BF16)
            rr = iota((sz.block, 128), 0)
            comp = (rr >= sz.plane).astype(jnp.int32) + (rr >= 2 * sz.plane).astype(jnp.int32)
            pm[...] = jnp.zeros_like(pm)
        for z in range(1, nz):
            here = pl.ds(sz.block * (z - 1), sz.block)
            level = (
                lev[it, 0, z, 0:sz.block].astype(F32) + lev[it, 1, z - 1, 0:sz.block].astype(F32)
            )
            bmat[here, :] = level.astype(BF16)
            if it == 0:
                names = (
                    lev[it, 0, z, sz.block:sz.level].astype(F32)
                    + lev[it, 1, z - 1, sz.block:sz.level].astype(F32)
                ).astype(BF16)
                col = 3.0 * dot(expand, names) + comp.astype(F32)
                col = jnp.where(rr < 3 * sz.plane, col, -1.0)
                for k in range(up_to(sz.coarse, 128) // 128):
                    width = min(128, sz.coarse - 128 * k)
                    at = (iota((sz.block, 128), 1) + 128 * k).astype(F32)
                    pm[here, 128 * k:128 * k + width] = (at == col).astype(F32).astype(BF16)[:, 0:width]
        if it == 0:
            loads[6].wait()
            pa[...] = dot(pm[...], inv[...]).astype(BF16)
            ae[0:sz.rows, :] = dot(pa[...], pm[...], (1, 1)).astype(BF16)
            ae[sz.rows:sz.rows + g_rows, :] = dot(ae[sz.rows:sz.rows + g_rows, :], ae[0:sz.rows, :]).astype(BF16)

        sol = dot(ae[...], bmat[...])
        coarse_part = jnp.sum(sol[0:sz.rows] * bmat[...].astype(F32), axis=0, keepdims=True)
        near = sol[sz.rows:]
        near_hi = near.astype(BF16)
        near_lo = (near - near_hi.astype(F32)).astype(BF16)

        total(0, sp.at[it], sp_send.at[it], sp_recv.at[it]).wait_recv()
        sums_now = mine + sp[it]
        gamma, cross, delta = sums_now[0:1], sums_now[1:2], sums_now[2:3] + coarse_part
        if it == 0:
            curve = delta
        else:
            beta = gamma / gamma_old
            curve = delta + 2.0 * beta * cross + beta * beta * curve
        alpha = gamma / curve
        gamma_old = gamma

        total(0, hn.at[it], h_send.at[it], h_recv.at[it]).wait_recv()
        for f in range(6):
            plus = f % 2
            if plus:
                a = f // 2
                if it == 0:
                    new = u[f]
                else:
                    new = u[f] + beta * p[a]
                if not last:
                    p[a] = new
                if it == 0:
                    x_ref[a] = alpha * new
                else:
                    x_ref[a] = x_ref[a] + alpha * new
            elif last:
                continue
            rows = slice(32 * (f + 1), 32 * (f + 2))
            cols = jnp.concatenate([near_hi[0:32], near_hi[rows], near_lo[0:32], near_lo[rows]], axis=0)
            jump = loc[face * f:face * f + face, :] - hn[it, f].astype(F32) + dot(wide_t[f], cols)
            new = (signs[f] * masks[f]) * jump
            if it:
                new = new + beta * s[f]
            if last:
                res_ref[f // 2] = r[f] - alpha * new
            else:
                s[f] = new
                r[f] = r[f] - alpha * new
                precondition(f)

    for copy in sent:
        copy.wait_send()
    for it in range(ITERS):
        tall = sz.level if it == 0 else sz.block
        total(0, rxy.at[it, pl.ds(0, sz.lines - 1)], xy_send.at[it], xy_recv.at[it]).wait_send()
        total(0, sx.at[it, pl.ds(0, sz.chips - 1)], sx_send.at[it], sx_recv.at[it]).wait_send()
        total(0, sy.at[it, pl.ds(0, nz - 1)], sy_send.at[it], sy_recv.at[it]).wait_send()
        total(0, sp.at[it], sp_send.at[it], sp_recv.at[it]).wait_send()
        total(0, lev.at[it, 0, pl.ds(0, nz - 1), pl.ds(0, tall)], z_send.at[it], z_recv.at[it]).wait_send()
        total(0, lev.at[it, 0, pl.ds(0, nz), pl.ds(0, tall)], pp_send.at[it], pp_recv.at[it]).wait_send()
        total(0, hn.at[it], h_send.at[it], h_recv.at[it]).wait_send()


def body(sz, dual_rhs, local_flex, corner_coupling, face_stiffness, coarse_inverse, corner_ids):
    nx, ny, nz = sz.grid
    face, dofs, cases = sz.face, sz.dofs, sz.cases
    vmem, dma = pltpu.VMEM, pltpu.SemaphoreType.DMA
    g_rows = 7 * 32
    it = ITERS
    scratch = [
        vmem((3, face, cases), F32), vmem((dofs, dofs), BF16), vmem((24, dofs), BF16),
        vmem((6, face, face), BF16), vmem((sz.coarse, sz.coarse), BF16),
        vmem((sz.level, sz.lines * 16), BF16), vmem((32, 24), BF16),
        vmem((3, face, cases), BF16), vmem((3, face, cases), BF16), vmem((6, face, face), BF16),
        vmem((32, sz.wide), BF16), vmem((6, 32, sz.window), BF16), vmem((sz.wide, 128), F32),
        vmem((sz.window, 128), F32), vmem((6, face, 128), BF16), vmem((6, face, face), BF16),
        vmem((6, face, cases), F32), vmem((6, face, cases), F32), vmem((6, face, cases), F32),
        vmem((3, face, cases), F32), vmem((dofs, cases), F32), vmem((sz.wide, cases), BF16),
        vmem((dofs, cases), F32), vmem((it, 2, 16, cases), BF16), vmem((it, sz.lines, 16, cases), BF16),
        vmem((it, 2, nz, sz.level, cases), BF16), vmem((it, 6, face, cases), BF16),
        vmem((it, 6, face, cases), BF16), vmem((sz.rows, cases), BF16),
        vmem((sz.rows + g_rows, sz.rows), BF16), vmem((sz.rows, sz.coarse), BF16),
        vmem((sz.rows, sz.coarse), BF16),
        vmem((it, 3, 8, cases), F32), vmem((it, sz.chips, 8, cases), F32),
        vmem((it, nz, 8, cases), F32), vmem((it, 8, cases), F32),
        dma((7,)), dma((15,)), dma((6,)), dma((3,)), dma((6,)),
    ] + [dma((it,)) for _ in range(14)]
    anywhere = pl.BlockSpec(memory_space=pl.ANY)
    whole = pl.BlockSpec(memory_space=pltpu.VMEM)
    out = jax.ShapeDtypeStruct((3, face, cases), F32)
    x, res = pl.pallas_call(
        functools.partial(kernel, sz),
        out_shape=(out, out),
        in_specs=[pl.BlockSpec(memory_space=pltpu.SMEM)] + [anywhere] * 7,
        out_specs=(whole, whole),
        scratch_shapes=scratch,
        compiler_params=pltpu.CompilerParams(
            collective_id=0, has_side_effects=True, vmem_limit_bytes=56 * 1024 * 1024
        ),
        name="dual_cg",
    )(
        corner_ids.reshape(8), dual_rhs.reshape(3, face, cases), local_flex.reshape(dofs, dofs),
        corner_coupling.reshape(24, dofs), face_stiffness.reshape(6, face, face), coarse_inverse,
        jnp.asarray(plane_sums(sz), BF16), jnp.asarray(corner_order(), BF16),
    )
    return x[None, None, None], res[None, None, None]


def solution(mesh):
    grid = (mesh.shape["gx"], mesh.shape["gy"], mesh.shape["gz"])

    def run(dual_rhs, local_flex, corner_coupling, face_stiffness, coarse_inverse, corner_ids):
        sz = Sizes(grid, dual_rhs.shape[4], dual_rhs.shape[5], coarse_inverse.shape[0])
        deep = P("gx", "gy", "gz", None, None, None)
        mid = P("gx", "gy", "gz", None, None)
        return jax.shard_map(
            functools.partial(body, sz),
            mesh=mesh,
            in_specs=(deep, mid, mid, deep, P(), P("gx", "gy", "gz", None)),
            out_specs=(deep, deep),
            check_vma=False,
        )(dual_rhs, local_flex, corner_coupling, face_stiffness, coarse_inverse, corner_ids)

    return run
```

time: 405 us -> 82.8 us (0.20)
  starting transfers between devices: 140 us -> 0 us
  blocking collectives: 133 us -> 0 us
  Pallas kernels: 0 us -> 75.6 us
  waiting for transfers between devices: 47.3 us -> 0 us
  local copies, waits for them, and re-layouts: 36.8 us -> 6.35 us
  matrix products: 29.4 us -> 0 us
  other arithmetic: 12.8 us -> 0 us
    all_to_all x11 -> x0, blocking collectives: 133 us -> none  [the longest x6 71.7 us: from_everyone(): return lax.all_to_all(copies, axis, split_axis=0, concat_axis=0, tiled=True)]
    pallas_call x0 -> x1, Pallas kernels: none -> 75.6 us  [body(): pl.pallas_call(functools.partial(kernel, sz), out_shape=(out, out), in_sp...]
    ppermute x27 -> x0, starting transfers between devices: 74.3 us -> none  [the longest x15 52.6 us: with_halo(): before = lax.ppermute(last, axis, up)]
    all_to_all x13 -> x0, starting transfers between devices: 66 us -> none  [the longest x12 59.5 us: from_everyone(): return lax.all_to_all(copies, axis, split_axis=0, concat_axis=0, tiled=True)]
    all_to_all x13 -> x0, waiting for transfers between devices: 37.1 us -> none  [the longest x12 33.6 us: from_everyone(): return lax.all_to_all(copies, axis, split_axis=0, concat_axis=0, tiled=True)]
    dot_general x24 -> x0, matrix products: 29.4 us -> none  [the longest x3 18 us: body(): jnp.dot(flex, signed, preferred_element_type=jnp.float32)]
    ppermute x27 -> x0, waiting for transfers between devices: 10.2 us -> none  [the longest x12 7.08 us: with_halo(): after = lax.ppermute(first, axis, down)]
    slice x11 -> x0, local copies, waits for them, and re-layouts: 8.52 us -> none  [the longest x3 2.55 us: with_halo(): last = lax.slice_in_dim(value, length - width, length, axis=dim)]
  transfers between devices with their start and end apart: 40 -> 0, of which waited for: 15 -> 0; matrix products, arithmetic and copies ran while one was open for 9% -> 0% of each run, Pallas kernels for 0% -> 0%
where the time goes in v1:
time: 82.8 us; the launch traced here: 82.6 us
  Pallas kernels  75.6 us (91%)
  local copies, waits for them, and re-layouts  6.35 us (8%)
    pallas_call x1, Pallas kernels, body(): pl.pallas_call(functools.partial(kernel, sz), out_shape=(out, out), in_sp...  75.6 us
    unnamed x3, local copies, waits for them, and re-layouts  6.35 us

profile of v1, /device:TPU:1, one launch (start us, length us, event | category | flops | bytes accessed | tf_op | source)
XLA Modules:
  0.0 82.6 jit_solution(1557270617661369949)
XLA Ops:
  0.6 1.8 %copy.14 = f32[1,1,1,3,300,128]{5,4,2,3,1,0:T(8,128)} copy(f32[1,1,1,3,300,128]{5,2,4,3,1,0:T(1,128)} %param.8) | data formatting | bytes 921600
  2.4 75.6 %dual_cg.1 = (f32[3,300,128]{2,1,0:T(8,128)}, f32[3,300,128]{2,1,0:T(8,128)}) custom-call(s32[8]{0:T(128)} %bitcast.15, f32[3,300,128]{2,1,0:T(8,128)} %bitcast.10, bf16[1800,1800]{1,0:T(8,128)(2,1)} %bitcast.9, bf16[24,1800]{1,0:T(8,128)(2,1)} %bitcast.14, bf16[6,300,300]{2,1,0:T(8,128)(2,1)} %bitcast.11, bf16[441,441]{1,0:T(8,128)(2,1)} %inv_h.1, ...), custom_call_target="tpu_custom_call" | custom-call | tf_op jit(solution)/shard_map/dual_cg/pallas_call | solution.py:408
  78.1 2.3 %copy.10 = f32[1,1,1,3,300,128]{5,2,4,3,1,0:T(1,128)} copy(f32[1,1,1,3,300,128]{5,4,3,2,1,0:T(8,128)} %bitcast.13) | data formatting | bytes 921600
  80.3 2.3 %copy.11 = f32[1,1,1,3,300,128]{5,2,4,3,1,0:T(1,128)} copy(f32[1,1,1,3,300,128]{5,4,3,2,1,0:T(8,128)} %bitcast.12) | data formatting | bytes 921600

commit v2 on v1

v2 whole, which is shorter than its diff:
```python
import functools

import jax
import jax.numpy as jnp
import numpy as np
from jax import lax
from jax.experimental import pallas as pl
from jax.experimental.pallas import tpu as pltpu
from jax.sharding import PartitionSpec as P

ITERS = 3
MESH = pl.DeviceIdType.MESH
F32 = jnp.float32
BF16 = jnp.bfloat16


def up_to(value, step):
    return -(-value // step) * step


def iota(shape, dim):
    return lax.broadcasted_iota(jnp.int32, shape, dim)


def dot(left, right, contract=None):
    if contract is None:
        contract = (left.ndim - 1, 0)
    dims = (((contract[0],), (contract[1],)), ((), ()))
    return lax.dot_general(left, right, dims, preferred_element_type=F32)


class Sizes:
    def __init__(self, grid, face, cases, coarse):
        self.grid, self.face, self.cases, self.coarse = grid, face, cases, coarse
        self.dofs = 6 * face
        self.window = up_to(face + 127, 128)
        self.wide = max(up_to(self.dofs, 128), face * 5 // 128 * 128 + self.window)
        self.split = face // 128 * 128
        self.rest = face - self.split
        self.tall = up_to(face, 16)
        nx, ny, nz = grid
        self.plane = (nx - 1) * (ny - 1)
        self.block = up_to(3 * self.plane + 1, 16)
        self.names = up_to(self.plane, 16)
        self.rows = up_to(self.block * (nz - 1), 128)
        self.lines = nx * ny


def plane_sums(sz):
    nx, ny, _ = sz.grid
    table = np.zeros((sz.block + sz.names, sz.lines * 16), np.float32)
    for i in range(nx):
        for j in range(ny):
            first = (i * ny + j) * 16
            for kx in range(2):
                for ky in range(2):
                    x, y = i + kx, j + ky
                    if not (1 <= x < nx and 1 <= y < ny):
                        continue
                    spot = (x - 1) * (ny - 1) + y - 1
                    for d in range(3):
                        table[d * sz.plane + spot, first + (kx * 2 + ky) * 3 + d] = 1
            if i + 1 < nx and j + 1 < ny:
                table[sz.block + i * (ny - 1) + j, first] = 1
    return table


def corner_order():
    table = np.zeros((32, 24), np.float32)
    for kx in range(2):
        for ky in range(2):
            for kz in range(2):
                for d in range(3):
                    row = kz * 16 + (kx * 2 + ky) * 3 + d
                    table[row, 3 * (4 * kx + 2 * ky + kz) + d] = 1
    return table


def kernel(sz, ids, rhs_h, flex_h, coup_h, stiff_h, inv_h, sums_h, order_h,
           x_h, res_h,
           rhs, flex, coup, stiff, inv, sums, order,
           rhs_b, rhs_n, t_b, t_n, kn, kc, kc_n, cs, cf, cn, own_t, nb_t, ksum, wg,
           r, s, t, u, p, x, sg, sgb, loc, wl, ml, cpb, rxy, lev, hb, hn, bmat, ae, pm, pa,
           idb, idr, idz, ss, sx, sy,
           load_sem, i_send, k_recv, kc_recv, r_recv, t_recv, c_recv,
           id_send, id_recv, idz_send, idz_recv, out_sem,
           xy_send, xy_recv, z_send, z_recv, pp_send, pp_recv, h_send, h_recv,
           sx_send, sx_recv, sy_send, sy_recv):
    nx, ny, nz = sz.grid
    face, dofs, split, rest, tall = sz.face, sz.dofs, sz.split, sz.rest, sz.tall
    i, j, l = lax.axis_index("gx"), lax.axis_index("gy"), lax.axis_index("gz")
    core = lax.rem(i, 2)
    place = (i, j, l)
    partner = {"gx": i + 1 - 2 * core, "gy": j, "gz": l}

    def toward(f):
        axis, step = f // 2, f % 2
        size = sz.grid[axis]
        spot = list(place)
        spot[axis] = lax.rem(spot[axis] + (1 if step else size - 1), size)
        return dict(zip(("gx", "gy", "gz"), spot))

    spread = sorted(
        [(di, dj) for di in range(nx) for dj in range(ny) if di or dj],
        key=lambda o: -(min(o[0], nx - o[0]) / 2 + min(o[1], ny - o[1])),
    )
    lanes = sorted(range(1, nz), key=lambda o: -min(o, nz - o))

    def across(di, dj):
        return {"gx": lax.rem(i + di, nx), "gy": lax.rem(j + dj, ny), "gz": l}

    def along(dl):
        return {"gx": i, "gy": j, "gz": lax.rem(l + dl, nz)}

    def remote(src, dst, send, recv, target):
        return pltpu.make_async_remote_copy(
            src_ref=src, dst_ref=dst, send_sem=send, recv_sem=recv,
            device_id=target, device_id_type=MESH,
        )

    def total(piece, send_sem, recv_sem):
        return remote(piece, piece, send_sem, recv_sem, partner)

    def send(src, dst, send_sem, recv_sem, target):
        copy = remote(src, dst, send_sem, recv_sem, target)
        copy.start()
        return copy

    loads = {}

    def load(name, src, dst):
        copy = pltpu.make_async_copy(src, dst, load_sem.at[len(loads)])
        copy.start()
        loads[name] = copy

    for a in range(3):
        load(("rhs", a), rhs_h.at[pl.ds(face * a, face), 0], rhs.at[a])
    for f in (1, 3, 5, 0, 2, 4):
        load(("stiff", f), stiff_h.at[f], stiff.at[f])
    load("coup", coup_h, coup)
    load("order", order_h, order)
    load("sums", sums_h, sums)
    load("flex", flex_h, flex)
    load("inv", inv_h, inv)

    barrier = pltpu.get_barrier_semaphore()
    for di, dj in spread:
        pl.semaphore_signal(barrier, inc=1, device_id=across(di, dj), device_id_type=MESH)
    for dl in lanes:
        pl.semaphore_signal(barrier, inc=1, device_id=along(dl), device_id_type=MESH)

    masks = []
    for f in range(6):
        axis, step = f // 2, f % 2
        edge = place[axis] < sz.grid[axis] - 1 if step else place[axis] > 0
        masks.append(jnp.where(edge, 1.0, 0.0).astype(F32))
    signs = [-1.0, 1.0] * 3

    for a in range(3):
        loads["rhs", a].wait()
        rhs_b[a] = rhs[a].astype(BF16)
        r[a] = rhs[a] * masks[2 * a + 1]
    for a in range(3):
        loads["stiff", 2 * a + 1].wait()
        t_b[a] = dot(stiff[2 * a + 1], rhs_b[a]).astype(BF16)
    kc[...] = jnp.zeros_like(kc)
    for f in (0, 2, 4, 1, 3, 5):
        if f % 2 == 0:
            loads["stiff", f].wait()
        kc[f, :, 0:rest] = stiff[f, split:face, split:face]
    idb[...] = jnp.full((16, sz.cases), ids[7], jnp.int32).astype(F32).astype(BF16)

    pl.semaphore_wait(barrier, len(spread) + len(lanes))

    sent = []

    def send_stiff(f):
        g = f ^ 1
        sent.append(send(stiff.at[f, :, pl.ds(0, split)], kn.at[g], i_send.at[f], k_recv.at[g], toward(f)))
        sent.append(send(kc.at[f], kc_n.at[g], i_send.at[6 + f], kc_recv.at[g], toward(f)))

    for a in range(3):
        sent.append(send(rhs_b.at[a], rhs_n.at[a], i_send.at[12 + a], r_recv.at[a], toward(2 * a + 1)))
        send_stiff(2 * a)
    for a in range(3):
        sent.append(send(t_b.at[a], t_n.at[a], i_send.at[15 + a], t_recv.at[a], toward(2 * a + 1)))
    slot = i * ny + j
    for di, dj in spread:
        send(idb, idr.at[slot], id_send, id_recv, across(di, dj))
    idr[slot] = idb[...]

    loads["coup"].wait()
    loads["order"].wait()
    cs[...] = jnp.zeros_like(cs)
    cs[:, 0:dofs] = dot(order[...], coup[...]).astype(BF16)
    starts = [face * f // 128 * 128 for f in range(6)]
    for f in range(6):
        off = face * f - starts[f]
        near = cs[:, starts[f]:starts[f] + sz.window].astype(F32)
        cf[f] = (signs[f] * near[:, off:off + face]).astype(BF16)
    pick_row, pick_col = iota((32, 128), 0), iota((32, 128), 1)
    pick_own = ((pick_col & 63) == pick_row).astype(F32).astype(BF16)
    pick_nb = -((pick_col & 63) == pick_row + 32).astype(F32).astype(BF16)
    own_t[...] = dot(cs[...], pick_own, (0, 0))

    g_rows = 7 * 32
    line = iota((g_rows, 128), 0)
    g, kz, e = line >> 5, (line >> 4) & 1, line & 15
    third = (e * 11) >> 5
    d, kx, ky = e - 3 * third, third >> 1, third & 1

    def shift(minus, plus):
        return (g == plus).astype(jnp.int32) - (g == minus).astype(jnp.int32)

    gx = i + kx + shift(1, 2)
    gy = j + ky + shift(3, 4)
    gz = l + kz + shift(5, 6)
    inside = (e < 12) & (gx >= 1) & (gx < nx) & (gy >= 1) & (gy < ny) & (gz >= 1) & (gz < nz)
    spot = jnp.where(
        inside, sz.block * (gz - 1) + sz.plane * d + (ny - 1) * (gx - 1) + gy - 1, -1
    )
    for k in range(sz.rows // 128):
        ae[sz.rows:sz.rows + g_rows, 128 * k:128 * k + 128] = (
            (iota((g_rows, 128), 1) + 128 * k == spot).astype(F32).astype(BF16)
        )
    bmat[...] = jnp.zeros_like(bmat)
    pm[...] = jnp.zeros_like(pm)
    wg[...] = jnp.zeros_like(wg)
    eye = (iota((rest, 128), 0) == iota((rest, 128), 1)).astype(F32).astype(BF16)

    def add_stiffness(f):
        for copy in (
            remote(kn.at[f], kn.at[f], i_send.at[f], k_recv.at[f], toward(f)),
            remote(kc.at[f], kc_n.at[f], i_send.at[6 + f], kc_recv.at[f], toward(f)),
        ):
            copy.wait_recv()
        both = (stiff[f, :, 0:split].astype(F32) + kn[f].astype(F32)).astype(BF16)
        ksum[f, :, 0:split] = both
        turned = dot(both[split:face], eye, (0, 0))
        ksum[f, 0:split, split:face] = turned[:, 0:rest].astype(BF16)
        ksum[f, split:face, split:face] = (
            stiff[f, split:face, split:face].astype(F32) + kc_n[f, :, 0:rest].astype(F32)
        ).astype(BF16)

    for a in range(3):
        remote(rhs_b.at[a], rhs_n.at[a], i_send.at[12 + a], r_recv.at[a], partner).wait_recv()
        part = dot(stiff[2 * a], rhs_n[a])
        add_stiffness(2 * a + 1)
        u[0, 2 * a + 1] = (0.25 * masks[2 * a + 1]) * dot(ksum[2 * a + 1], rhs_b[a])
        remote(t_b.at[a], t_n.at[a], i_send.at[15 + a], t_recv.at[a], partner).wait_recv()
        u[0, 2 * a] = (0.25 * masks[2 * a]) * (part + t_n[a].astype(F32))

    alpha = beta = gamma_old = curve = None
    for it in range(ITERS):
        last = it + 1 == ITERS
        now, then = it % 2, (it + 1) % 2
        cp = None
        for f in range(6):
            piece = dot(cf[f], u[now, f].astype(BF16))
            cp = piece if cp is None else cp + piece
        low, high = cp[0:16].astype(BF16), cp[16:32].astype(BF16)
        cpb[it, 0] = low
        cpb[it, 1] = high
        for di, dj in spread:
            target = across(di, dj)
            send(cpb.at[it, lax.rem(target["gx"], 2)], rxy.at[it, slot], xy_send.at[it],
                 xy_recv.at[it], target)
        rxy[it, slot] = jnp.where(core == 0, low.astype(F32), high.astype(F32)).astype(BF16)
        if it == 0:
            for f in (1, 3, 5):
                send_stiff(f)
            for f in range(6):
                sent.append(
                    send(cs.at[:, pl.ds(starts[f], sz.window)], cn.at[f ^ 1], i_send.at[18 + f],
                         c_recv.at[f ^ 1], toward(f))
                )
            total(idr.at[pl.ds(0, sz.lines - 1)], id_send, id_recv).wait_recv()
            loads["sums"].wait()
            idz[l] = dot(sums[sz.block:], idr[...].reshape(sz.lines * 16, sz.cases)).astype(BF16)
            for dl in lanes:
                send(idz.at[l], idz.at[l], idz_send, idz_recv, along(dl))

        for f in range(6):
            sg[face * f:face * f + face, :] = signs[f] * u[now, f]
        sgb[...] = sg[...].astype(BF16)
        if it == 0:
            loads["flex"].wait()
        loc[...] = dot(flex[...], sgb[...])
        delta = jnp.sum(sgb[...].astype(F32) * loc[...], axis=0, keepdims=True)
        for a in range(3):
            f = 2 * a + 1
            if it == 0:
                continue
            new = u[then, f]
            if it > 1:
                new = new + beta * p[a]
            p[a] = new
            x[a] = alpha * new if it == 1 else x[a] + alpha * new
            r[a] = r[a] - alpha * s[a]
        gamma = sum(jnp.sum(r[a] * u[now, 2 * a + 1], axis=0, keepdims=True) for a in range(3))
        if it:
            cross = sum(jnp.sum(s[a] * u[now, 2 * a + 1], axis=0, keepdims=True) for a in range(3))
        else:
            cross = jnp.zeros_like(gamma)
        where = iota((4, sz.cases), 0)
        packed = jnp.where(where == 0, gamma, jnp.where(where == 1, cross, jnp.where(where == 2, delta, 0.0)))
        ss[it, 0] = packed
        sx[it, slot] = packed
        for di, dj in spread:
            send(ss.at[it, 0], sx.at[it, slot], sx_send.at[it], sx_recv.at[it], across(di, dj))
        for f in range(6):
            hb[it, f] = loc[face * f:face * f + face, :].astype(BF16)
            send(hb.at[it, f], hn.at[it, f ^ 1], h_send.at[it], h_recv.at[it], toward(f))

        total(rxy.at[it, pl.ds(0, sz.lines - 1)], xy_send.at[it], xy_recv.at[it]).wait_recv()
        lev[it, core, l] = dot(sums[0:sz.block], rxy[it].reshape(sz.lines * 16, sz.cases)).astype(BF16)
        for dl in lanes:
            piece = lev.at[it, core, l]
            send(piece, piece, z_send.at[it], z_recv.at[it], along(dl))

        total(hn.at[it], h_send.at[it], h_recv.at[it]).wait_recv()

        def local_jump(f):
            jump = (signs[f] * masks[f]) * (loc[face * f:face * f + face, :] - hn[it, f].astype(F32))
            if f % 2:
                wl[f // 2] = jump
            if not last:
                ml[f] = (0.25 * masks[f]) * dot(ksum[f], jump.astype(BF16))

        for f in (1, 3, 5) if it == 0 or last else range(6):
            local_jump(f)

        total(sx.at[it, pl.ds(0, sz.lines - 1)], sx_send.at[it], sx_recv.at[it]).wait_recv()
        packed = jnp.sum(sx[it], axis=0)
        ss[it, 1] = packed
        sy[it, l] = packed
        for dl in lanes:
            send(ss.at[it, 1], sy.at[it, l], sy_send.at[it], sy_recv.at[it], along(dl))

        if it == 0:
            for f in (0, 2, 4):
                add_stiffness(f)
                local_jump(f)
            for f in range(6):
                remote(cs.at[:, pl.ds(starts[f], sz.window)], cn.at[f], i_send.at[18 + f],
                       c_recv.at[f], toward(f)).wait_recv()
                nb_t[...] = dot(cn[f], pick_nb, (0, 0))
                off = face * (f ^ 1) - starts[f ^ 1]
                wide = (signs[f] * masks[f]) * (own_t[face * f:face * f + face, :] + nb_t[off:off + face, :])
                wide = wide.astype(BF16)
                wg[f, 0:face, :] = wide
                wg[f, tall:tall + face, :] = ((0.25 * masks[f]) * dot(ksum[f], wide)).astype(BF16)

            small_r, small_c = iota((sz.block, sz.names), 0), iota((sz.block, sz.names), 1)
            part = (small_r >= sz.plane).astype(jnp.int32) + (small_r >= 2 * sz.plane).astype(jnp.int32)
            expand = ((small_c == small_r - sz.plane * part) & (small_r < 3 * sz.plane)).astype(F32).astype(BF16)
            rr = iota((sz.block, 128), 0)
            comp = (rr >= sz.plane).astype(jnp.int32) + (rr >= 2 * sz.plane).astype(jnp.int32)
            total(idz.at[pl.ds(0, nz - 1)], idz_send, idz_recv).wait_recv()
            for z in range(1, nz):
                here = pl.ds(sz.block * (z - 1), sz.block)
                col = 3.0 * dot(expand, idz[z - 1]) + comp.astype(F32)
                col = jnp.where(rr < 3 * sz.plane, col, -1.0)
                for k in range(up_to(sz.coarse, 128) // 128):
                    width = min(128, sz.coarse - 128 * k)
                    at = (iota((sz.block, 128), 1) + 128 * k).astype(F32)
                    pm[here, 128 * k:128 * k + width] = (at == col).astype(F32).astype(BF16)[:, 0:width]
            loads["inv"].wait()
            pa[...] = dot(pm[...], inv[...]).astype(BF16)
            ae[0:sz.rows, :] = dot(pa[...], pm[...], (1, 1)).astype(BF16)
            ae[sz.rows:sz.rows + g_rows, :] = dot(ae[sz.rows:sz.rows + g_rows, :], ae[0:sz.rows, :]).astype(BF16)

        total(lev.at[it, 0, pl.ds(0, nz - 1)], z_send.at[it], z_recv.at[it]).wait_recv()
        piece = lev.at[it, core]
        send(piece, piece, pp_send.at[it], pp_recv.at[it], partner)
        total(piece, pp_send.at[it], pp_recv.at[it]).wait_recv()

        for z in range(1, nz):
            level = lev[it, 0, z].astype(F32) + lev[it, 1, z - 1].astype(F32)
            bmat[sz.block * (z - 1):sz.block * z, :] = level.astype(BF16)
        sol = dot(ae[...], bmat[...])
        coarse_part = jnp.sum(sol[0:sz.rows] * bmat[...].astype(F32), axis=0, keepdims=True)
        near = sol[sz.rows:]
        near_hi = near.astype(BF16)
        near_lo = (near - near_hi.astype(F32)).astype(BF16)

        total(sy.at[it, pl.ds(0, nz - 1)], sy_send.at[it], sy_recv.at[it]).wait_recv()
        sums_now = jnp.sum(sy[it], axis=0)
        gamma, cross, delta = sums_now[0:1], sums_now[1:2], sums_now[2:3] + coarse_part
        if it == 0:
            curve = delta
        else:
            beta = gamma / gamma_old
            curve = delta + 2.0 * beta * cross + beta * beta * curve
        alpha = gamma / curve
        gamma_old = gamma

        for f in (1, 3, 5) if last else range(6):
            rows = slice(32 * (f + 1), 32 * (f + 2))
            cols = jnp.concatenate([near_hi[0:32], near_hi[rows], near_lo[0:32], near_lo[rows]], axis=0)
            a = f // 2
            if last:
                new = wl[a] + dot(wg[f, 0:face, :], cols) + beta * s[a]
                res = r[a] - alpha * new
                sum_p = u[now, f] + beta * p[a]
                r[a] = res
                x[a] = x[a] + alpha * sum_p
                continue
            both = dot(wg[f], cols)
            turned = ml[f] + both[tall:tall + face]
            if it:
                turned = turned + beta * t[f]
            t[f] = turned
            u[then, f] = u[now, f] - alpha * turned
            if f % 2:
                new = wl[a] + both[0:face]
                s[a] = new if it == 0 else new + beta * s[a]

    outs = []
    for a in range(3):
        for n, (src, dst) in enumerate(((x, x_h), (r, res_h))):
            copy = pltpu.make_async_copy(src.at[a], dst.at[pl.ds(face * a, face), 0], out_sem.at[n, a])
            copy.start()
            outs.append(copy)
    for copy in sent:
        copy.wait_send()
    total(idr.at[pl.ds(0, sz.lines - 1)], id_send, id_recv).wait_send()
    total(idz.at[pl.ds(0, nz - 1)], idz_send, idz_recv).wait_send()
    for it in range(ITERS):
        total(rxy.at[it, pl.ds(0, sz.lines - 1)], xy_send.at[it], xy_recv.at[it]).wait_send()
        total(sx.at[it, pl.ds(0, sz.lines - 1)], sx_send.at[it], sx_recv.at[it]).wait_send()
        total(sy.at[it, pl.ds(0, nz - 1)], sy_send.at[it], sy_recv.at[it]).wait_send()
        total(lev.at[it, 0, pl.ds(0, nz - 1)], z_send.at[it], z_recv.at[it]).wait_send()
        total(lev.at[it, 0], pp_send.at[it], pp_recv.at[it]).wait_send()
        total(hn.at[it], h_send.at[it], h_recv.at[it]).wait_send()
    for copy in outs:
        copy.wait()


def body(sz, dual_rhs, local_flex, corner_coupling, face_stiffness, coarse_inverse, corner_ids):
    nx, ny, nz = sz.grid
    face, dofs, cases = sz.face, sz.dofs, sz.cases
    vmem, dma = pltpu.VMEM, pltpu.SemaphoreType.DMA
    g_rows = 7 * 32
    it = ITERS
    scratch = [
        vmem((3, face, cases), F32), vmem((dofs, dofs), BF16), vmem((24, dofs), BF16),
        vmem((6, face, face), BF16), vmem((sz.coarse, sz.coarse), BF16),
        vmem((sz.block + sz.names, sz.lines * 16), BF16), vmem((32, 24), BF16),
        vmem((3, face, cases), BF16), vmem((3, face, cases), BF16),
        vmem((3, face, cases), BF16), vmem((3, face, cases), BF16),
        vmem((6, face, sz.split), BF16), vmem((6, sz.rest, 128), BF16), vmem((6, sz.rest, 128), BF16),
        vmem((32, sz.wide), BF16), vmem((6, 32, face), BF16), vmem((6, 32, sz.window), BF16),
        vmem((sz.wide, 128), F32), vmem((sz.window, 128), F32), vmem((6, face, face), BF16),
        vmem((6, 2 * sz.tall, 128), BF16),
        vmem((3, face, cases), F32), vmem((3, face, cases), F32), vmem((6, face, cases), F32),
        vmem((2, 6, face, cases), F32), vmem((3, face, cases), F32), vmem((3, face, cases), F32),
        vmem((dofs, cases), F32), vmem((dofs, cases), BF16), vmem((dofs, cases), F32),
        vmem((3, face, cases), F32), vmem((6, face, cases), F32),
        vmem((it, 2, 16, cases), BF16), vmem((it, sz.lines, 16, cases), BF16),
        vmem((it, 2, nz, sz.block, cases), BF16), vmem((it, 6, face, cases), BF16),
        vmem((it, 6, face, cases), BF16), vmem((sz.rows, cases), BF16),
        vmem((sz.rows + g_rows, sz.rows), BF16), vmem((sz.rows, sz.coarse), BF16),
        vmem((sz.rows, sz.coarse), BF16),
        vmem((16, cases), BF16), vmem((sz.lines, 16, cases), BF16), vmem((nz, sz.names, cases), BF16),
        vmem((it, 2, 4, cases), F32), vmem((it, sz.lines, 4, cases), F32), vmem((it, nz, 4, cases), F32),
        dma((14,)), dma((24,)), dma((6,)), dma((6,)), dma((3,)), dma((3,)), dma((6,)),
        dma, dma, dma, dma, dma((2, 3)),
    ] + [dma((it,)) for _ in range(12)]
    anywhere = pl.BlockSpec(memory_space=pl.ANY)
    out = jax.ShapeDtypeStruct((3 * face, 1, cases), F32)
    x, res = pl.pallas_call(
        functools.partial(kernel, sz),
        out_shape=(out, out),
        in_specs=[pl.BlockSpec(memory_space=pltpu.SMEM)] + [anywhere] * 7,
        out_specs=(anywhere, anywhere),
        scratch_shapes=scratch,
        compiler_params=pltpu.CompilerParams(
            collective_id=0, has_side_effects=True, vmem_limit_bytes=56 * 1024 * 1024
        ),
        name="dual_cg",
    )(
        corner_ids.reshape(8), dual_rhs.reshape(3 * face, 1, cases), local_flex.reshape(dofs, dofs),
        corner_coupling.reshape(24, dofs), face_stiffness.reshape(6, face, face), coarse_inverse,
        jnp.asarray(plane_sums(sz), BF16), jnp.asarray(corner_order(), BF16),
    )
    shape = (1, 1, 1, 3, face, cases)
    return x.reshape(shape), res.reshape(shape)


def solution(mesh):
    grid = (mesh.shape["gx"], mesh.shape["gy"], mesh.shape["gz"])

    def run(dual_rhs, local_flex, corner_coupling, face_stiffness, coarse_inverse, corner_ids):
        sz = Sizes(grid, dual_rhs.shape[4], dual_rhs.shape[5], coarse_inverse.shape[0])
        deep = P("gx", "gy", "gz", None, None, None)
        mid = P("gx", "gy", "gz", None, None)
        return jax.shard_map(
            functools.partial(body, sz),
            mesh=mesh,
            in_specs=(deep, mid, mid, deep, P(), P("gx", "gy", "gz", None)),
            out_specs=(deep, deep),
            check_vma=False,
        )(dual_rhs, local_flex, corner_coupling, face_stiffness, coarse_inverse, corner_ids)

    return run
```

time: 82.8 us -> 75.2 us (0.908)
  Pallas kernels: 75.6 us -> 70.7 us
  local copies, waits for them, and re-layouts: 6.35 us -> 3.64 us
    pallas_call x1, Pallas kernels: 75.6 us -> 70.7 us  [body(): pl.pallas_call(functools.partial(kernel, sz), out_shape=(out, out), in_sp...]
    unnamed x3 -> x2, local copies, waits for them, and re-layouts: 6.35 us -> 3.64 us
where the time goes in v2:
time: 75.2 us; the launch traced here: 75 us
  Pallas kernels  70.7 us (94%)
  local copies, waits for them, and re-layouts  3.64 us (5%)
    pallas_call x1, Pallas kernels, body(): pl.pallas_call(functools.partial(kernel, sz), out_shape=(out, out), in_sp...  70.7 us
    unnamed x2, local copies, waits for them, and re-layouts  3.64 us

profile of v2, /device:TPU:1, one launch (start us, length us, event | category | flops | bytes accessed | tf_op | source)
XLA Modules:
  0.0 75.0 jit_solution(7103469197988150187)
XLA Ops:
  0.6 70.7 %dual_cg.1 = (f32[900,1,128]{2,1,0:T(1,128)}, f32[900,1,128]{2,1,0:T(1,128)}) custom-call(s32[8]{0:T(128)} %bitcast.17, f32[900,1,128]{2,1,0:T(1,128)} %bitcast.13, bf16[1800,1800]{1,0:T(8,128)(2,1)} %bitcast.11, bf16[24,1800]{1,0:T(8,128)(2,1)} %bitcast.16, bf16[6,300,300]{2,1,0:T(8,128)(2,1)} %bitcast.12, bf16[441,441]{1,0:T(8,128)(2,1)} %inv_h.1, ...), custom_call_target="tpu_custom_call" | custom-call | tf_op jit(solution)/shard_map/dual_cg/pallas_call | solution.py:472
  71.3 1.8 %copy.14 = f32[1,1,1,3,300,128]{5,2,4,3,1,0:T(1,128)} copy(f32[1,1,1,3,300,128]{5,2,4,3,1,0:T(1,128)} %bitcast.15) | data formatting | bytes 921600
  73.1 1.8 %copy.15 = f32[1,1,1,3,300,128]{5,2,4,3,1,0:T(1,128)} copy(f32[1,1,1,3,300,128]{5,2,4,3,1,0:T(1,128)} %bitcast.14) | data formatting | bytes 921600

commit v3 on v2

--- a/solution.py
+++ b/solution.py
@@ -48,7 +48,8 @@
 
 def plane_sums(sz):
     nx, ny, _ = sz.grid
-    table = np.zeros((sz.block + sz.names, sz.lines * 16), np.float32)
+    table = np.zeros((sz.block, sz.lines * 16), np.float32)
+    names = np.zeros((sz.names, sz.lines * 8), np.float32)
     for i in range(nx):
         for j in range(ny):
             first = (i * ny + j) * 16
@@ -61,8 +62,8 @@
                     for d in range(3):
                         table[d * sz.plane + spot, first + (kx * 2 + ky) * 3 + d] = 1
             if i + 1 < nx and j + 1 < ny:
-                table[sz.block + i * (ny - 1) + j, first] = 1
-    return table
+                names[i * (ny - 1) + j, first // 2] = 1
+    return table, names
 
 
 def corner_order():
@@ -76,14 +77,14 @@
     return table
 
 
-def kernel(sz, ids, rhs_h, flex_h, coup_h, stiff_h, inv_h, sums_h, order_h,
-           x_h, res_h,
-           rhs, flex, coup, stiff, inv, sums, order,
+def kernel(sz, ids_h, rhs_h, flex_h, coup_h, stiff_h, inv_h, sums_h, sums_n_h, order_h,
+           x, r,
+           ids, rhs, flex, coup, stiff, inv, sums, sums_n, order,
            rhs_b, rhs_n, t_b, t_n, kn, kc, kc_n, cs, cf, cn, own_t, nb_t, ksum, wg,
-           r, s, t, u, p, x, sg, sgb, loc, wl, ml, cpb, rxy, lev, hb, hn, bmat, ae, pm, pa,
+           s, t, u, p, sg, sgb, loc, wl, ml, cpb, rxy, lev, hb, hn, bmat, ae, pm, pa,
            idb, idr, idz, ss, sx, sy,
            load_sem, i_send, k_recv, kc_recv, r_recv, t_recv, c_recv,
-           id_send, id_recv, idz_send, idz_recv, out_sem,
+           id_send, id_recv, idz_send, idz_recv,
            xy_send, xy_recv, z_send, z_recv, pp_send, pp_recv, h_send, h_recv,
            sx_send, sx_recv, sy_send, sy_recv):
     nx, ny, nz = sz.grid
@@ -133,6 +134,7 @@
         copy.start()
         loads[name] = copy
 
+    load("ids", ids_h, ids)
     for a in range(3):
         load(("rhs", a), rhs_h.at[pl.ds(face * a, face), 0], rhs.at[a])
     for f in (1, 3, 5, 0, 2, 4):
@@ -140,6 +142,7 @@
     load("coup", coup_h, coup)
     load("order", order_h, order)
     load("sums", sums_h, sums)
+    load("sums_n", sums_n_h, sums_n)
     load("flex", flex_h, flex)
     load("inv", inv_h, inv)
 
@@ -168,7 +171,8 @@
         if f % 2 == 0:
             loads["stiff", f].wait()
         kc[f, :, 0:rest] = stiff[f, split:face, split:face]
-    idb[...] = jnp.full((16, sz.cases), ids[7], jnp.int32).astype(F32).astype(BF16)
+    loads["ids"].wait()
+    idb[...] = jnp.full((8, sz.cases), ids[7], jnp.int32).astype(F32).astype(BF16)
 
     pl.semaphore_wait(barrier, len(spread) + len(lanes))
 
@@ -194,6 +198,13 @@
     cs[...] = jnp.zeros_like(cs)
     cs[:, 0:dofs] = dot(order[...], coup[...]).astype(BF16)
     starts = [face * f // 128 * 128 for f in range(6)]
+    for f in range(6):
+        sent.append(
+            send(cs.at[:, pl.ds(starts[f], sz.window)], cn.at[f ^ 1], i_send.at[18 + f],
+                 c_recv.at[f ^ 1], toward(f))
+        )
+    for f in (1, 3, 5):
+        send_stiff(f)
     for f in range(6):
         off = face * f - starts[f]
         near = cs[:, starts[f]:starts[f] + sz.window].astype(F32)
@@ -267,16 +278,10 @@
                  xy_recv.at[it], target)
         rxy[it, slot] = jnp.where(core == 0, low.astype(F32), high.astype(F32)).astype(BF16)
         if it == 0:
-            for f in (1, 3, 5):
-                send_stiff(f)
-            for f in range(6):
-                sent.append(
-                    send(cs.at[:, pl.ds(starts[f], sz.window)], cn.at[f ^ 1], i_send.at[18 + f],
-                         c_recv.at[f ^ 1], toward(f))
-                )
             total(idr.at[pl.ds(0, sz.lines - 1)], id_send, id_recv).wait_recv()
             loads["sums"].wait()
-            idz[l] = dot(sums[sz.block:], idr[...].reshape(sz.lines * 16, sz.cases)).astype(BF16)
+            loads["sums_n"].wait()
+            idz[l] = dot(sums_n[...], idr[...].reshape(sz.lines * 8, sz.cases)).astype(BF16)
             for dl in lanes:
                 send(idz.at[l], idz.at[l], idz_send, idz_recv, along(dl))
 
@@ -312,35 +317,9 @@
             hb[it, f] = loc[face * f:face * f + face, :].astype(BF16)
             send(hb.at[it, f], hn.at[it, f ^ 1], h_send.at[it], h_recv.at[it], toward(f))
 
-        total(rxy.at[it, pl.ds(0, sz.lines - 1)], xy_send.at[it], xy_recv.at[it]).wait_recv()
-        lev[it, core, l] = dot(sums[0:sz.block], rxy[it].reshape(sz.lines * 16, sz.cases)).astype(BF16)
-        for dl in lanes:
-            piece = lev.at[it, core, l]
-            send(piece, piece, z_send.at[it], z_recv.at[it], along(dl))
-
-        total(hn.at[it], h_send.at[it], h_recv.at[it]).wait_recv()
-
-        def local_jump(f):
-            jump = (signs[f] * masks[f]) * (loc[face * f:face * f + face, :] - hn[it, f].astype(F32))
-            if f % 2:
-                wl[f // 2] = jump
-            if not last:
-                ml[f] = (0.25 * masks[f]) * dot(ksum[f], jump.astype(BF16))
-
-        for f in (1, 3, 5) if it == 0 or last else range(6):
-            local_jump(f)
-
-        total(sx.at[it, pl.ds(0, sz.lines - 1)], sx_send.at[it], sx_recv.at[it]).wait_recv()
-        packed = jnp.sum(sx[it], axis=0)
-        ss[it, 1] = packed
-        sy[it, l] = packed
-        for dl in lanes:
-            send(ss.at[it, 1], sy.at[it, l], sy_send.at[it], sy_recv.at[it], along(dl))
-
         if it == 0:
             for f in (0, 2, 4):
                 add_stiffness(f)
-                local_jump(f)
             for f in range(6):
                 remote(cs.at[:, pl.ds(starts[f], sz.window)], cn.at[f], i_send.at[18 + f],
                        c_recv.at[f], toward(f)).wait_recv()
@@ -351,6 +330,13 @@
                 wg[f, 0:face, :] = wide
                 wg[f, tall:tall + face, :] = ((0.25 * masks[f]) * dot(ksum[f], wide)).astype(BF16)
 
+        total(rxy.at[it, pl.ds(0, sz.lines - 1)], xy_send.at[it], xy_recv.at[it]).wait_recv()
+        lev[it, core, l] = dot(sums[...], rxy[it].reshape(sz.lines * 16, sz.cases)).astype(BF16)
+        for dl in lanes:
+            piece = lev.at[it, core, l]
+            send(piece, piece, z_send.at[it], z_recv.at[it], along(dl))
+
+        if it == 0:
             small_r, small_c = iota((sz.block, sz.names), 0), iota((sz.block, sz.names), 1)
             part = (small_r >= sz.plane).astype(jnp.int32) + (small_r >= 2 * sz.plane).astype(jnp.int32)
             expand = ((small_c == small_r - sz.plane * part) & (small_r < 3 * sz.plane)).astype(F32).astype(BF16)
@@ -369,6 +355,25 @@
             pa[...] = dot(pm[...], inv[...]).astype(BF16)
             ae[0:sz.rows, :] = dot(pa[...], pm[...], (1, 1)).astype(BF16)
             ae[sz.rows:sz.rows + g_rows, :] = dot(ae[sz.rows:sz.rows + g_rows, :], ae[0:sz.rows, :]).astype(BF16)
+
+        total(hn.at[it], h_send.at[it], h_recv.at[it]).wait_recv()
+
+        def local_jump(f):
+            jump = (signs[f] * masks[f]) * (loc[face * f:face * f + face, :] - hn[it, f].astype(F32))
+            if f % 2:
+                wl[f // 2] = jump
+            if not last:
+                ml[f] = (0.25 * masks[f]) * dot(ksum[f], jump.astype(BF16))
+
+        for f in (1, 3, 5) if last else range(6):
+            local_jump(f)
+
+        total(sx.at[it, pl.ds(0, sz.lines - 1)], sx_send.at[it], sx_recv.at[it]).wait_recv()
+        packed = jnp.sum(sx[it], axis=0)
+        ss[it, 1] = packed
+        sy[it, l] = packed
+        for dl in lanes:
+            send(ss.at[it, 1], sy.at[it, l], sy_send.at[it], sy_recv.at[it], along(dl))
 
         total(lev.at[it, 0, pl.ds(0, nz - 1)], z_send.at[it], z_recv.at[it]).wait_recv()
         piece = lev.at[it, core]
@@ -416,12 +421,6 @@
                 new = wl[a] + both[0:face]
                 s[a] = new if it == 0 else new + beta * s[a]
 
-    outs = []
-    for a in range(3):
-        for n, (src, dst) in enumerate(((x, x_h), (r, res_h))):
-            copy = pltpu.make_async_copy(src.at[a], dst.at[pl.ds(face * a, face), 0], out_sem.at[n, a])
-            copy.start()
-            outs.append(copy)
     for copy in sent:
         copy.wait_send()
     total(idr.at[pl.ds(0, sz.lines - 1)], id_send, id_recv).wait_send()
@@ -433,6 +432,15 @@
         total(lev.at[it, 0, pl.ds(0, nz - 1)], z_send.at[it], z_recv.at[it]).wait_send()
         total(lev.at[it, 0], pp_send.at[it], pp_recv.at[it]).wait_send()
         total(hn.at[it], h_send.at[it], h_recv.at[it]).wait_send()
+
+
+def deliver(face, x, r, x_h, r_h, sem):
+    outs = []
+    for a in range(3):
+        for n, (src, dst) in enumerate(((x, x_h), (r, r_h))):
+            copy = pltpu.make_async_copy(src.at[a], dst.at[pl.ds(face * a, face), 0], sem.at[n, a])
+            copy.start()
+            outs.append(copy)
     for copy in outs:
         copy.wait()
 
@@ -444,17 +452,17 @@
     g_rows = 7 * 32
     it = ITERS
     scratch = [
-        vmem((3, face, cases), F32), vmem((dofs, dofs), BF16), vmem((24, dofs), BF16),
+        pltpu.SMEM((8,), jnp.int32), vmem((3, face, cases), F32), vmem((dofs, dofs), BF16), vmem((24, dofs), BF16),
         vmem((6, face, face), BF16), vmem((sz.coarse, sz.coarse), BF16),
-        vmem((sz.block + sz.names, sz.lines * 16), BF16), vmem((32, 24), BF16),
+        vmem((sz.block, sz.lines * 16), BF16), vmem((sz.names, sz.lines * 8), BF16), vmem((32, 24), BF16),
         vmem((3, face, cases), BF16), vmem((3, face, cases), BF16),
         vmem((3, face, cases), BF16), vmem((3, face, cases), BF16),
         vmem((6, face, sz.split), BF16), vmem((6, sz.rest, 128), BF16), vmem((6, sz.rest, 128), BF16),
         vmem((32, sz.wide), BF16), vmem((6, 32, face), BF16), vmem((6, 32, sz.window), BF16),
         vmem((sz.wide, 128), F32), vmem((sz.window, 128), F32), vmem((6, face, face), BF16),
         vmem((6, 2 * sz.tall, 128), BF16),
-        vmem((3, face, cases), F32), vmem((3, face, cases), F32), vmem((6, face, cases), F32),
-        vmem((2, 6, face, cases), F32), vmem((3, face, cases), F32), vmem((3, face, cases), F32),
+        vmem((3, face, cases), F32), vmem((6, face, cases), F32),
+        vmem((2, 6, face, cases), F32), vmem((3, face, cases), F32),
         vmem((dofs, cases), F32), vmem((dofs, cases), BF16), vmem((dofs, cases), F32),
         vmem((3, face, cases), F32), vmem((6, face, cases), F32),
         vmem((it, 2, 16, cases), BF16), vmem((it, sz.lines, 16, cases), BF16),
@@ -462,18 +470,20 @@
         vmem((it, 6, face, cases), BF16), vmem((sz.rows, cases), BF16),
         vmem((sz.rows + g_rows, sz.rows), BF16), vmem((sz.rows, sz.coarse), BF16),
         vmem((sz.rows, sz.coarse), BF16),
-        vmem((16, cases), BF16), vmem((sz.lines, 16, cases), BF16), vmem((nz, sz.names, cases), BF16),
+        vmem((8, cases), BF16), vmem((sz.lines, 8, cases), BF16), vmem((nz, sz.names, cases), BF16),
         vmem((it, 2, 4, cases), F32), vmem((it, sz.lines, 4, cases), F32), vmem((it, nz, 4, cases), F32),
-        dma((14,)), dma((24,)), dma((6,)), dma((6,)), dma((3,)), dma((3,)), dma((6,)),
-        dma, dma, dma, dma, dma((2, 3)),
+        dma((16,)), dma((24,)), dma((6,)), dma((6,)), dma((3,)), dma((3,)), dma((6,)),
+        dma, dma, dma, dma,
     ] + [dma((it,)) for _ in range(12)]
     anywhere = pl.BlockSpec(memory_space=pl.ANY)
+    whole = pl.BlockSpec(memory_space=pltpu.VMEM)
+    held = pltpu.VMEM((3, face, cases), F32)
     out = jax.ShapeDtypeStruct((3 * face, 1, cases), F32)
     x, res = pl.pallas_call(
         functools.partial(kernel, sz),
-        out_shape=(out, out),
-        in_specs=[pl.BlockSpec(memory_space=pltpu.SMEM)] + [anywhere] * 7,
-        out_specs=(anywhere, anywhere),
+        out_shape=(held, held),
+        in_specs=[anywhere] * 9,
+        out_specs=(whole, whole),
         scratch_shapes=scratch,
         compiler_params=pltpu.CompilerParams(
             collective_id=0, has_side_effects=True, vmem_limit_bytes=56 * 1024 * 1024
@@ -482,8 +492,16 @@
     )(
         corner_ids.reshape(8), dual_rhs.reshape(3 * face, 1, cases), local_flex.reshape(dofs, dofs),
         corner_coupling.reshape(24, dofs), face_stiffness.reshape(6, face, face), coarse_inverse,
-        jnp.asarray(plane_sums(sz), BF16), jnp.asarray(corner_order(), BF16),
+        *(jnp.asarray(table, BF16) for table in (*plane_sums(sz), corner_order())),
     )
+    x, res = pl.pallas_call(
+        functools.partial(deliver, face),
+        out_shape=(out, out),
+        in_specs=[whole, whole],
+        out_specs=(anywhere, anywhere),
+        scratch_shapes=[dma((2, 3))],
+        name="deliver",
+    )(*(pltpu.with_memory_space_constraint(v, pltpu.VMEM) for v in (x, res)))
     shape = (1, 1, 1, 3, face, cases)
     return x.reshape(shape), res.reshape(shape)
 

time: 75.2 us -> 68 us (0.904)
  local copies, waits for them, and re-layouts: 3.64 us -> 0 us
  Pallas kernels: 70.7 us -> 67.2 us
    unnamed x2 -> x0, local copies, waits for them, and re-layouts: 3.64 us -> none
    pallas_call x1 -> x2, Pallas kernels: 70.7 us -> 67.2 us  [the longest x1 66.2 us: body(): pl.pallas_call(functools.partial(kernel, sz), out_shape=(held, held), in_...]
where the time goes in v3:
time: 68 us
  Pallas kernels  67.2 us (99%)
  between operations  0.8 us (1%)
    pallas_call x1, Pallas kernels, body(): pl.pallas_call(functools.partial(kernel, sz), out_shape=(held, held), in_...  66.2 us

profile of v3, /device:TPU:1, one launch (start us, length us, event | category | flops | bytes accessed | tf_op | source)
XLA Modules:
  0.0 68.0 jit_solution(3886374728847252868)
XLA Ops:
  0.6 66.2 %dual_cg.1 = (f32[3,300,128]{2,1,0:T(8,128)S(1)}, f32[3,300,128]{2,1,0:T(8,128)S(1)}) custom-call(s32[8]{0:T(128)} %bitcast.15, f32[900,1,128]{2,1,0:T(1,128)} %bitcast.13, bf16[1800,1800]{1,0:T(8,128)(2,1)} %bitcast.11, bf16[24,1800]{1,0:T(8,128)(2,1)} %bitcast.14, bf16[6,300,300]{2,1,0:T(8,128)(2,1)} %bitcast.12, bf16[441,441]{1,0:T(8,128)(2,1)} %inv_h.1, ...), custom_call_target="tpu_custom_call" | custom-call | tf_op jit(solution)/shard_map/dual_cg/pallas_call | solution.py:482
  66.8 1.0 %deliver.1 = (f32[900,1,128]{2,1,0:T(1,128)}, f32[900,1,128]{2,1,0:T(1,128)}) custom-call(f32[3,300,128]{2,1,0:T(8,128)S(1)} %get-tuple-element.6.x, f32[3,300,128]{2,1,0:T(8,128)S(1)} %get-tuple-element.7.r), custom_call_target="tpu_custom_call" | custom-call | tf_op jit(solution)/shard_map/deliver/pallas_call | solution.py:497

commit v4 on v3

--- a/solution.py
+++ b/solution.py
@@ -261,14 +261,19 @@
         remote(t_b.at[a], t_n.at[a], i_send.at[15 + a], t_recv.at[a], partner).wait_recv()
         u[0, 2 * a] = (0.25 * masks[2 * a]) * (part + t_n[a].astype(F32))
 
-    alpha = beta = gamma_old = curve = None
+    def corner_part(value):
+        part = None
+        for f in range(6):
+            piece = dot(cf[f], value(f).astype(BF16))
+            part = piece if part is None else part + piece
+        return part
+
+    alpha = beta = gamma_old = curve = cp = cp_turned = None
     for it in range(ITERS):
         last = it + 1 == ITERS
         now, then = it % 2, (it + 1) % 2
-        cp = None
-        for f in range(6):
-            piece = dot(cf[f], u[now, f].astype(BF16))
-            cp = piece if cp is None else cp + piece
+        if it == 0:
+            cp = corner_part(lambda f: u[0, f])
         low, high = cp[0:16].astype(BF16), cp[16:32].astype(BF16)
         cpb[it, 0] = low
         cpb[it, 1] = high
@@ -286,22 +291,19 @@
                 send(idz.at[l], idz.at[l], idz_send, idz_recv, along(dl))
 
         for f in range(6):
+            if it:
+                t[f] = ml[f] if it == 1 else ml[f] + beta * t[f]
+                u[now, f] = u[then, f] - alpha * t[f]
             sg[face * f:face * f + face, :] = signs[f] * u[now, f]
         sgb[...] = sg[...].astype(BF16)
         if it == 0:
             loads["flex"].wait()
         loc[...] = dot(flex[...], sgb[...])
         delta = jnp.sum(sgb[...].astype(F32) * loc[...], axis=0, keepdims=True)
-        for a in range(3):
-            f = 2 * a + 1
-            if it == 0:
-                continue
-            new = u[then, f]
-            if it > 1:
-                new = new + beta * p[a]
-            p[a] = new
-            x[a] = alpha * new if it == 1 else x[a] + alpha * new
-            r[a] = r[a] - alpha * s[a]
+        if it:
+            for a in range(3):
+                s[a] = wl[a] if it == 1 else wl[a] + beta * s[a]
+                r[a] = r[a] - alpha * s[a]
         gamma = sum(jnp.sum(r[a] * u[now, 2 * a + 1], axis=0, keepdims=True) for a in range(3))
         if it:
             cross = sum(jnp.sum(s[a] * u[now, 2 * a + 1], axis=0, keepdims=True) for a in range(3))
@@ -313,9 +315,16 @@
         sx[it, slot] = packed
         for di, dj in spread:
             send(ss.at[it, 0], sx.at[it, slot], sx_send.at[it], sx_recv.at[it], across(di, dj))
-        for f in range(6):
+        for f in (0, 2, 4) if last else range(6):
             hb[it, f] = loc[face * f:face * f + face, :].astype(BF16)
             send(hb.at[it, f], hn.at[it, f ^ 1], h_send.at[it], h_recv.at[it], toward(f))
+        if it:
+            for a in range(3):
+                new = u[then, 2 * a + 1]
+                if it > 1:
+                    new = new + beta * p[a]
+                p[a] = new
+                x[a] = alpha * new if it == 1 else x[a] + alpha * new
 
         if it == 0:
             for f in (0, 2, 4):
@@ -335,6 +344,25 @@
         for dl in lanes:
             piece = lev.at[it, core, l]
             send(piece, piece, z_send.at[it], z_recv.at[it], along(dl))
+
+        total(hn.at[it, pl.ds(0, 3)] if last else hn.at[it], h_send.at[it], h_recv.at[it]).wait_recv()
+
+        def local_jump(f):
+            jump = (signs[f] * masks[f]) * (loc[face * f:face * f + face, :] - hn[it, f].astype(F32))
+            if f % 2:
+                wl[f // 2] = jump
+            if not last:
+                ml[f] = (0.25 * masks[f]) * dot(ksum[f], jump.astype(BF16))
+
+        for f in (1, 3, 5) if last else range(6):
+            local_jump(f)
+
+        total(sx.at[it, pl.ds(0, sz.lines - 1)], sx_send.at[it], sx_recv.at[it]).wait_recv()
+        packed = jnp.sum(sx[it], axis=0)
+        ss[it, 1] = packed
+        sy[it, l] = packed
+        for dl in lanes:
+            send(ss.at[it, 1], sy.at[it, l], sy_send.at[it], sy_recv.at[it], along(dl))
 
         if it == 0:
             small_r, small_c = iota((sz.block, sz.names), 0), iota((sz.block, sz.names), 1)
@@ -356,25 +384,6 @@
             ae[0:sz.rows, :] = dot(pa[...], pm[...], (1, 1)).astype(BF16)
             ae[sz.rows:sz.rows + g_rows, :] = dot(ae[sz.rows:sz.rows + g_rows, :], ae[0:sz.rows, :]).astype(BF16)
 
-        total(hn.at[it], h_send.at[it], h_recv.at[it]).wait_recv()
-
-        def local_jump(f):
-            jump = (signs[f] * masks[f]) * (loc[face * f:face * f + face, :] - hn[it, f].astype(F32))
-            if f % 2:
-                wl[f // 2] = jump
-            if not last:
-                ml[f] = (0.25 * masks[f]) * dot(ksum[f], jump.astype(BF16))
-
-        for f in (1, 3, 5) if last else range(6):
-            local_jump(f)
-
-        total(sx.at[it, pl.ds(0, sz.lines - 1)], sx_send.at[it], sx_recv.at[it]).wait_recv()
-        packed = jnp.sum(sx[it], axis=0)
-        ss[it, 1] = packed
-        sy[it, l] = packed
-        for dl in lanes:
-            send(ss.at[it, 1], sy.at[it, l], sy_send.at[it], sy_recv.at[it], along(dl))
-
         total(lev.at[it, 0, pl.ds(0, nz - 1)], z_send.at[it], z_recv.at[it]).wait_recv()
         piece = lev.at[it, core]
         send(piece, piece, pp_send.at[it], pp_recv.at[it], partner)
@@ -389,6 +398,21 @@
         near_hi = near.astype(BF16)
         near_lo = (near - near_hi.astype(F32)).astype(BF16)
 
+        def columns(f):
+            rows = slice(32 * (f + 1), 32 * (f + 2))
+            return jnp.concatenate([near_hi[0:32], near_hi[rows], near_lo[0:32], near_lo[rows]], axis=0)
+
+        if last:
+            for a in range(3):
+                f = 2 * a + 1
+                wl[a] = wl[a] + dot(wg[f, 0:face, :], columns(f))
+        else:
+            for f in range(6):
+                both = dot(wg[f], columns(f))
+                ml[f] = ml[f] + both[tall:tall + face]
+                if f % 2:
+                    wl[f // 2] = wl[f // 2] + both[0:face]
+            turned = corner_part(lambda f: ml[f])
         total(sy.at[it, pl.ds(0, nz - 1)], sy_send.at[it], sy_recv.at[it]).wait_recv()
         sums_now = jnp.sum(sy[it], axis=0)
         gamma, cross, delta = sums_now[0:1], sums_now[1:2], sums_now[2:3] + coarse_part
@@ -400,26 +424,13 @@
         alpha = gamma / curve
         gamma_old = gamma
 
-        for f in (1, 3, 5) if last else range(6):
-            rows = slice(32 * (f + 1), 32 * (f + 2))
-            cols = jnp.concatenate([near_hi[0:32], near_hi[rows], near_lo[0:32], near_lo[rows]], axis=0)
-            a = f // 2
-            if last:
-                new = wl[a] + dot(wg[f, 0:face, :], cols) + beta * s[a]
-                res = r[a] - alpha * new
-                sum_p = u[now, f] + beta * p[a]
-                r[a] = res
-                x[a] = x[a] + alpha * sum_p
-                continue
-            both = dot(wg[f], cols)
-            turned = ml[f] + both[tall:tall + face]
-            if it:
-                turned = turned + beta * t[f]
-            t[f] = turned
-            u[then, f] = u[now, f] - alpha * turned
-            if f % 2:
-                new = wl[a] + both[0:face]
-                s[a] = new if it == 0 else new + beta * s[a]
+        if last:
+            for a in range(3):
+                r[a] = r[a] - alpha * (wl[a] + beta * s[a])
+                x[a] = x[a] + alpha * (u[now, 2 * a + 1] + beta * p[a])
+        else:
+            cp_turned = turned if it == 0 else turned + beta * cp_turned
+            cp = cp - alpha * cp_turned
 
     for copy in sent:
         copy.wait_send()
@@ -431,7 +442,8 @@
         total(sy.at[it, pl.ds(0, nz - 1)], sy_send.at[it], sy_recv.at[it]).wait_send()
         total(lev.at[it, 0, pl.ds(0, nz - 1)], z_send.at[it], z_recv.at[it]).wait_send()
         total(lev.at[it, 0], pp_send.at[it], pp_recv.at[it]).wait_send()
-        total(hn.at[it], h_send.at[it], h_recv.at[it]).wait_send()
+        part = hn.at[it, pl.ds(0, 3)] if it + 1 == ITERS else hn.at[it]
+        total(part, h_send.at[it], h_recv.at[it]).wait_send()
 
 
 def deliver(face, x, r, x_h, r_h, sem):

time: 68 us -> 65.5 us (0.963)
  Pallas kernels: 67.2 us -> 64.2 us
    pallas_call x1, Pallas kernels: 66.2 us -> 63.2 us  [body(): pl.pallas_call(functools.partial(kernel, sz), out_shape=(held, held), in_...]
where the time goes in v4:
time: 65.5 us; the launch traced here: 65 us
  Pallas kernels  64.2 us (98%)
  between operations  0.8 us (1%)
    pallas_call x1, Pallas kernels, body(): pl.pallas_call(functools.partial(kernel, sz), out_shape=(held, held), in_...  63.2 us

profile of v4, /device:TPU:1, one launch (start us, length us, event | category | flops | bytes accessed | tf_op | source)
XLA Modules:
  0.0 65.0 jit_solution(18437944074022123804)
XLA Ops:
  0.6 63.2 %dual_cg.1 = (f32[3,300,128]{2,1,0:T(8,128)S(1)}, f32[3,300,128]{2,1,0:T(8,128)S(1)}) custom-call(s32[8]{0:T(128)} %bitcast.15, f32[900,1,128]{2,1,0:T(1,128)} %bitcast.13, bf16[1800,1800]{1,0:T(8,128)(2,1)} %bitcast.11, bf16[24,1800]{1,0:T(8,128)(2,1)} %bitcast.14, bf16[6,300,300]{2,1,0:T(8,128)(2,1)} %bitcast.12, bf16[441,441]{1,0:T(8,128)(2,1)} %inv_h.1, ...), custom_call_target="tpu_custom_call" | custom-call | tf_op jit(solution)/shard_map/dual_cg/pallas_call | solution.py:494
  63.9 1.0 %deliver.1 = (f32[900,1,128]{2,1,0:T(1,128)}, f32[900,1,128]{2,1,0:T(1,128)}) custom-call(f32[3,300,128]{2,1,0:T(8,128)S(1)} %get-tuple-element.6.x, f32[3,300,128]{2,1,0:T(8,128)S(1)} %get-tuple-element.7.r), custom_call_target="tpu_custom_call" | custom-call | tf_op jit(solution)/shard_map/deliver/pallas_call | solution.py:509

commit v5 on v4

--- a/solution.py
+++ b/solution.py
@@ -345,6 +345,13 @@
             piece = lev.at[it, core, l]
             send(piece, piece, z_send.at[it], z_recv.at[it], along(dl))
 
+        total(sx.at[it, pl.ds(0, sz.lines - 1)], sx_send.at[it], sx_recv.at[it]).wait_recv()
+        packed = jnp.sum(sx[it], axis=0)
+        ss[it, 1] = packed
+        sy[it, l] = packed
+        for dl in lanes:
+            send(ss.at[it, 1], sy.at[it, l], sy_send.at[it], sy_recv.at[it], along(dl))
+
         total(hn.at[it, pl.ds(0, 3)] if last else hn.at[it], h_send.at[it], h_recv.at[it]).wait_recv()
 
         def local_jump(f):
@@ -356,13 +363,6 @@
 
         for f in (1, 3, 5) if last else range(6):
             local_jump(f)
-
-        total(sx.at[it, pl.ds(0, sz.lines - 1)], sx_send.at[it], sx_recv.at[it]).wait_recv()
-        packed = jnp.sum(sx[it], axis=0)
-        ss[it, 1] = packed
-        sy[it, l] = packed
-        for dl in lanes:
-            send(ss.at[it, 1], sy.at[it, l], sy_send.at[it], sy_recv.at[it], along(dl))
 
         if it == 0:
             small_r, small_c = iota((sz.block, sz.names), 0), iota((sz.block, sz.names), 1)

time: 65.5 us -> 64.3 us (0.982)
  Pallas kernels: 64.2 us -> 63.4 us
    pallas_call x1, Pallas kernels: 63.2 us -> 62.4 us  [body(): pl.pallas_call(functools.partial(kernel, sz), out_shape=(held, held), in_...]
where the time goes in v5:
time: 64.3 us; the launch traced here: 64.2 us
  Pallas kernels  63.4 us (99%)
  between operations  0.8 us (1%)
    pallas_call x1, Pallas kernels, body(): pl.pallas_call(functools.partial(kernel, sz), out_shape=(held, held), in_...  62.4 us

profile of v5, /device:TPU:1, one launch (start us, length us, event | category | flops | bytes accessed | tf_op | source)
XLA Modules:
  0.0 64.2 jit_solution(4016926071312351146)
XLA Ops:
  0.6 62.4 %dual_cg.1 = (f32[3,300,128]{2,1,0:T(8,128)S(1)}, f32[3,300,128]{2,1,0:T(8,128)S(1)}) custom-call(s32[8]{0:T(128)} %bitcast.15, f32[900,1,128]{2,1,0:T(1,128)} %bitcast.13, bf16[1800,1800]{1,0:T(8,128)(2,1)} %bitcast.11, bf16[24,1800]{1,0:T(8,128)(2,1)} %bitcast.14, bf16[6,300,300]{2,1,0:T(8,128)(2,1)} %bitcast.12, bf16[441,441]{1,0:T(8,128)(2,1)} %inv_h.1, ...), custom_call_target="tpu_custom_call" | custom-call | tf_op jit(solution)/shard_map/dual_cg/pallas_call | solution.py:494
  63.1 1.0 %deliver.1 = (f32[900,1,128]{2,1,0:T(1,128)}, f32[900,1,128]{2,1,0:T(1,128)}) custom-call(f32[3,300,128]{2,1,0:T(8,128)S(1)} %get-tuple-element.6.x, f32[3,300,128]{2,1,0:T(8,128)S(1)} %get-tuple-element.7.r), custom_call_target="tpu_custom_call" | custom-call | tf_op jit(solution)/shard_map/deliver/pallas_call | solution.py:509
